TPU v7x, 32 devices: a whole 2x2x4 slice. The times are simulated.
32 devices in a mesh: dp: 16 (over z, y, x), tensor: 2 (over core).
Axes of the slice: x: 2, y: 2, z: 4, core: 2. Of those that a mesh axis runs over, the one named last changes fastest.
Arguments:
- vis_rows: bfloat16 [8, 128, 2, 3200], P(None, 'dp', None, 'tensor'), may hold values from -6 to 6
- ln_gain: float32 [2, 3200], replicated, may hold values from 0.25 to 1.75
- ln_bias: float32 [2, 3200], replicated, may hold values from -3 to 3
- proj_weight: bfloat16 [3200, 2, 8192], P('dp', None, 'tensor'), may hold values from -0.078125 to 0.078125
- text_rows: bfloat16 [16, 384, 8192], P('dp', None, 'tensor'), may hold values from -8 to 8
- attn_gain: float32 [8192], replicated, may hold values from 0.25 to 1.75
- w_query: bfloat16 [8192, 4096], P('dp', 'tensor'), may hold values from -0.088388348 to 0.088388348
- key_value_weight: bfloat16 [8192, 2, 1024], P('dp', None, 'tensor'), may hold values from -0.088388348 to 0.088388348
- tile_counts: int32 [16], replicated, may hold values from 1 to 16, 128 in all
- image_offsets: int32 [16], P('dp'), may hold values from 0 to 256
Outputs:
- attn_context: bfloat16 [16, 384, 4096], P('dp', None, 'tensor')
Inputs may be any that keep to these rules, and one draw needn't show every extreme that they name: tile_counts counts all 128 tiles, and its largest entry is exactly 16.
All inputs are finite; a program needn't handle non-finite values.
Results may differ from a plain program's by a relative error of at most 0.0074.
Values may be sent and summed in bfloat16 or wider, within the bound.
A program may use at most 128 MiB of HBM per device.

v0:
```python
import functools
import math

import jax
import jax.numpy as jnp
from jax import lax
from jax.experimental import pallas as pl
from jax.experimental.pallas import tpu as pltpu
from jax.sharding import PartitionSpec as P

QUERY_HEADS = 32
KEY_VALUE_HEADS = 8
HEAD_WIDTH = 128


vision_epsilon = 1e-06
decoder_epsilon = 1e-05
rope_base = 500000.0


def layer_norm(value_rows, gain, bias_values):
    average = jnp.mean(value_rows, axis=(-2, -1), keepdims=True)
    centered = value_rows - average
    variance = jnp.mean(centered * centered, axis=(-2, -1), keepdims=True)
    return centered * lax.rsqrt(variance + vision_epsilon) * gain + bias_values


MESH = pl.DeviceIdType.MESH


def partner(data_index, step, inner, plane):
    if plane is None:
        return lax.rem(data_index + step, inner)
    outer_at, inner_at = data_index // inner, data_index % inner
    if plane:
        return outer_at * inner + lax.rem(inner_at + step, inner)
    count = lax.axis_size("dp") // inner
    return lax.rem(outer_at + step, count) * inner + inner_at


def place(data_index, inner, plane):
    if plane is None:
        return data_index
    return data_index % inner if plane else data_index // inner


def greet(size, inner, plane):
    data_index = lax.axis_index("dp")
    barrier = pltpu.get_barrier_semaphore()
    for step in range(1, size):
        pl.semaphore_signal(
            barrier,
            inc=1,
            device_id={"dp": partner(data_index, step, inner, plane)},
            device_id_type=MESH,
        )
    pl.semaphore_wait(barrier, size - 1)


def exchange_kernel(size, inner, plane, x_ref, o_ref, send_sem, recv_sem, own_sem):
    data_index = lax.axis_index("dp")
    me = place(data_index, inner, plane)
    own = pltpu.make_async_copy(x_ref.at[me], o_ref.at[me], own_sem)
    own.start()
    greet(size, inner, plane)
    copies = []
    for step in range(1, size):
        target = partner(data_index, step, inner, plane)
        copy = pltpu.make_async_remote_copy(
            src_ref=x_ref.at[place(target, inner, plane)],
            dst_ref=o_ref.at[me],
            send_sem=send_sem.at[step - 1],
            recv_sem=recv_sem.at[step - 1],
            device_id={"dp": target},
            device_id_type=MESH,
        )
        copy.start()
        copies.append(copy)
    own.wait()
    for copy in copies:
        copy.wait()


def greet_both(inner):
    data_index = lax.axis_index("dp")
    outer = lax.axis_size("dp") // inner
    barrier = pltpu.get_barrier_semaphore()
    for plane, size in ((True, inner), (False, outer)):
        for step in range(1, size):
            pl.semaphore_signal(
                barrier,
                inc=1,
                device_id={"dp": partner(data_index, step, inner, plane)},
                device_id_type=MESH,
            )
    pl.semaphore_wait(barrier, inner + outer - 2)


def reduce_kernel(
    inner, chunks, rows, x_ref, o_ref, held, mid, got, send_1, recv_1, send_2, recv_2
):
    data_index = lax.axis_index("dp")
    outer, tokens, columns = mid.shape
    wide = columns // chunks
    me, me_outer = place(data_index, inner, True), place(data_index, inner, False)
    greet_both(inner)
    first, second = {}, {}
    for chunk in range(chunks):
        part = pl.ds(chunk * wide, wide)
        for step in range(1, inner):
            target = partner(data_index, step, inner, True)
            first[chunk, step] = pltpu.make_async_remote_copy(
                src_ref=x_ref.at[:, place(target, inner, True), :, part],
                dst_ref=held.at[step - 1, :, :, part],
                send_sem=send_1.at[step - 1, chunk],
                recv_sem=recv_1.at[step - 1, chunk],
                device_id={"dp": target},
                device_id_type=MESH,
            )
            first[chunk, step].start()
    for chunk in range(chunks):
        part = pl.ds(chunk * wide, wide)
        for step in range(1, inner):
            first[chunk, step].wait_recv()

        def add(at, carry):
            row = lax.rem(me_outer + 1 + at // (tokens // rows), outer)
            window = pl.ds(pl.multiple_of(at % (tokens // rows) * rows, rows), rows)
            total = x_ref[row, me, window, part].astype(jnp.float32)
            for step in range(1, inner):
                total = total + held[step - 1, row, window, part].astype(jnp.float32)
            mid[row, window, part] = total.astype(mid.dtype)
            return carry

        lax.fori_loop(0, outer * (tokens // rows), add, 0)
        for step in range(1, outer):
            target = partner(data_index, step, inner, False)
            second[chunk, step] = pltpu.make_async_remote_copy(
                src_ref=mid.at[place(target, inner, False), :, part],
                dst_ref=got.at[step - 1, :, part],
                send_sem=send_2.at[step - 1, chunk],
                recv_sem=recv_2.at[step - 1, chunk],
                device_id={"dp": target},
                device_id_type=MESH,
            )
            second[chunk, step].start()
    for chunk in range(chunks):
        part = pl.ds(chunk * wide, wide)
        for step in range(1, outer):
            second[chunk, step].wait_recv()

        def finish(at, carry):
            window = pl.ds(pl.multiple_of(at * rows, rows), rows)
            total = mid[me_outer, window, part].astype(jnp.float32)
            for step in range(1, outer):
                total = total + got[step - 1, window, part].astype(jnp.float32)
            o_ref[window, part] = total.astype(o_ref.dtype)
            return carry

        lax.fori_loop(0, tokens // rows, finish, 0)
    for copy in list(first.values()) + list(second.values()):
        copy.wait_send()


def reduce_blocks(partial, number):
    outer, inner, tokens, columns = partial.shape
    chunks = 4
    return pl.pallas_call(
        functools.partial(reduce_kernel, inner, chunks, math.gcd(tokens, 16)),
        out_shape=jax.ShapeDtypeStruct((tokens, columns), partial.dtype),
        in_specs=[pl.BlockSpec(memory_space=pltpu.VMEM)],
        out_specs=pl.BlockSpec(memory_space=pltpu.VMEM),
        scratch_shapes=[
            pltpu.VMEM((inner - 1, outer, tokens, columns), partial.dtype),
            pltpu.VMEM((outer, tokens, columns), partial.dtype),
            pltpu.VMEM((outer - 1, tokens, columns), partial.dtype),
            pltpu.SemaphoreType.DMA((inner - 1, chunks)),
            pltpu.SemaphoreType.DMA((inner - 1, chunks)),
            pltpu.SemaphoreType.DMA((outer - 1, chunks)),
            pltpu.SemaphoreType.DMA((outer - 1, chunks)),
        ],
        compiler_params=pltpu.CompilerParams(
            collective_id=number, has_side_effects=True, vmem_limit_bytes=40 << 20
        ),
        cost_estimate=pl.CostEstimate(
            flops=0, bytes_accessed=60 * partial.size, transcendentals=0
        ),
    )(partial)


def product_kernel(inner, count, tile, rows, *refs):
    a_refs = refs[:count]
    w_ref, o_ref, leaving, held, send_sem, recv_sem = refs[count:]
    depth = w_ref.shape[0] // count
    tensor_index = lax.axis_index("tensor")
    data_index = lax.axis_index("dp")
    tiles = o_ref.shape[1] // tile

    def compute(block, dst_ref, low, high):
        def one(at, carry):
            part = pl.ds(pl.multiple_of(at * tile, tile), tile)
            total = None
            for ahead, a_ref in enumerate(a_refs):
                start = lax.rem(tensor_index + count - ahead, count) * depth
                rows_at = pl.ds(pl.multiple_of(start, depth), depth)
                term = jnp.dot(
                    a_ref[block], w_ref[rows_at, part], preferred_element_type=jnp.float32
                )
                total = term if total is None else total + term
            dst_ref[:, part] = total.astype(dst_ref.dtype)
            return carry

        lax.fori_loop(low, high, one, 0)

    greet(inner, inner, True)
    copies = []
    for step in range(1, inner + 1):
        target = partner(data_index, step, inner, True)
        block = place(target, inner, True)
        dst_ref = leaving.at[step - 1] if step < inner else o_ref
        compute(block, dst_ref, 0, 1)
        if copies:
            copies[-1].start()
        compute(block, dst_ref, 1, tiles)
        if step < inner:
            copies.append(
                pltpu.make_async_remote_copy(
                    src_ref=leaving.at[step - 1],
                    dst_ref=held.at[step - 1],
                    send_sem=send_sem.at[step - 1],
                    recv_sem=recv_sem.at[step - 1],
                    device_id={"dp": target},
                    device_id_type=MESH,
                )
            )
    for copy in copies:
        copy.wait_recv()

    def add(at, carry):
        window = pl.ds(pl.multiple_of(at * rows, rows), rows)
        total = o_ref[window, :]
        for step in range(1, inner):
            total = total + held[step - 1, window, :].astype(jnp.float32)
        o_ref[window, :] = total
        return carry

    lax.fori_loop(0, o_ref.shape[0] // rows, add, 0)
    for copy in copies:
        copy.wait_send()


def product_blocks(pieces, weight, number):
    inner, rows, depth = pieces[0].shape
    columns = weight.shape[1]
    count = len(pieces)
    return pl.pallas_call(
        functools.partial(
            product_kernel, inner, count, math.gcd(columns, 512), math.gcd(rows, 16)
        ),
        out_shape=jax.ShapeDtypeStruct((rows, columns), jnp.float32),
        in_specs=[pl.BlockSpec(memory_space=pltpu.VMEM)] * (count + 1),
        out_specs=pl.BlockSpec(memory_space=pltpu.VMEM),
        scratch_shapes=[
            pltpu.VMEM((inner - 1, rows, columns), jnp.bfloat16),
            pltpu.VMEM((inner - 1, rows, columns), jnp.bfloat16),
            pltpu.SemaphoreType.DMA((inner - 1,)),
            pltpu.SemaphoreType.DMA((inner - 1,)),
        ],
        compiler_params=pltpu.CompilerParams(
            collective_id=number, has_side_effects=True, vmem_limit_bytes=56 << 20
        ),
        cost_estimate=pl.CostEstimate(
            flops=2 * count * inner * rows * depth * columns,
            bytes_accessed=200 << 20,
            transcendentals=0,
        ),
    )(*pieces, weight)


def exchange(blocks, inner, plane, number):
    size = blocks.shape[0]
    return pl.pallas_call(
        functools.partial(exchange_kernel, size, inner, plane),
        out_shape=jax.ShapeDtypeStruct(blocks.shape, blocks.dtype),
        in_specs=[pl.BlockSpec(memory_space=pltpu.VMEM)],
        out_specs=pl.BlockSpec(memory_space=pltpu.VMEM),
        scratch_shapes=[
            pltpu.SemaphoreType.DMA((size - 1,)),
            pltpu.SemaphoreType.DMA((size - 1,)),
            pltpu.SemaphoreType.DMA,
        ],
        compiler_params=pltpu.CompilerParams(
            collective_id=number, has_side_effects=True, vmem_limit_bytes=40 << 20
        ),
        cost_estimate=pl.CostEstimate(
            flops=0, bytes_accessed=40 * blocks.size, transcendentals=0
        ),
    )(blocks)


def tensor_pieces(block):
    count = lax.axis_size("tensor")
    pieces = [block]
    for step in range(1, count):
        ring = [(at, (at + step) % count) for at in range(count)]
        pieces.append(lax.ppermute(block, "tensor", ring))
    return pieces


def attend_kernel(group, q_ref, k_ref, v_ref, cos_ref, sin_ref, o_ref):
    cosine, sine = cos_ref[...], sin_ref[...]

    def turn(rows):
        return (rows * cosine + pltpu.roll(rows, HEAD_WIDTH // 2, 1) * sine).astype(jnp.bfloat16)

    key_rows = turn(k_ref[...])
    value_rows = v_ref[...].astype(jnp.bfloat16)
    seq_len = key_rows.shape[0]
    row_at = lax.broadcasted_iota(jnp.int32, (seq_len, seq_len), 0)
    column_at = lax.broadcasted_iota(jnp.int32, (seq_len, seq_len), 1)
    for head in range(group):
        part = pl.ds(head * HEAD_WIDTH, HEAD_WIDTH)
        query_rows = turn(q_ref[:, part])
        scores = lax.dot_general(
            query_rows, key_rows, (((1,), (1,)), ((), ())), preferred_element_type=jnp.float32
        ) * HEAD_WIDTH ** (-0.5)
        scores = jnp.where(row_at >= column_at, scores, -1e30)
        exponentials = jnp.exp(scores - jnp.max(scores, axis=-1, keepdims=True))
        weights = exponentials / jnp.sum(exponentials, axis=-1, keepdims=True)
        context = jnp.dot(
            weights.astype(jnp.bfloat16), value_rows, preferred_element_type=jnp.float32
        )
        o_ref[:, part] = context.astype(o_ref.dtype)


def attend(product, part_query):
    seq_len, columns = product.shape
    group = QUERY_HEADS // KEY_VALUE_HEADS
    local_kv = part_query // HEAD_WIDTH // group
    key_at = part_query // HEAD_WIDTH
    half_width = HEAD_WIDTH // 2
    exponents = jnp.arange(half_width, dtype=jnp.float32) * (2.0 / HEAD_WIDTH)
    frequency = rope_base ** (-exponents)
    angles = jnp.arange(seq_len, dtype=jnp.float32)[:, None] * frequency[None, :]
    cosine, sine = jnp.cos(angles), jnp.sin(angles)
    cosine = jnp.concatenate([cosine, cosine], axis=1)
    sine = jnp.concatenate([-sine, sine], axis=1)
    table = pl.BlockSpec((seq_len, HEAD_WIDTH), lambda g: (0, 0))
    return pl.pallas_call(
        functools.partial(attend_kernel, group),
        grid=(local_kv,),
        out_shape=jax.ShapeDtypeStruct((seq_len, part_query), jnp.bfloat16),
        in_specs=[
            pl.BlockSpec((seq_len, group * HEAD_WIDTH), lambda g: (0, g)),
            pl.BlockSpec((seq_len, HEAD_WIDTH), lambda g: (0, key_at + g)),
            pl.BlockSpec((seq_len, HEAD_WIDTH), lambda g: (0, key_at + local_kv + g)),
            table,
            table,
        ],
        out_specs=pl.BlockSpec((seq_len, group * HEAD_WIDTH), lambda g: (0, g)),
        compiler_params=pltpu.CompilerParams(vmem_limit_bytes=24 << 20),
    )(product, product, product, cosine, sine)


def per_device(
    vis_rows,
    ln_gain,
    ln_bias,
    proj_weight,
    text_rows,
    attn_gain,
    w_query,
    key_value_weight,
    tile_counts,
    image_offsets,
):
    data_count = lax.axis_size("dp")
    data_index = lax.axis_index("dp")
    tensor_count = lax.axis_size("tensor")
    tensor_index = lax.axis_index("tensor")
    tile_rows, tile_tok, merge_count, part_width = vis_rows.shape
    vision_width = ln_gain.shape[1]
    part_model = proj_weight.shape[2]
    token_count = tile_rows * tile_tok
    inner = 1 << (int(math.log2(data_count)) // 2)
    outer = data_count // inner
    columns_of = [[at * inner + b for at in range(outer)] for b in range(inner)]
    depth = w_query.shape[0]
    weight = jnp.concatenate([w_query, key_value_weight.reshape(depth, -1)], axis=1)
    weight = lax.all_gather(weight, "dp", axis=0, tiled=True, axis_index_groups=columns_of)

    max_tiles = 2 * tile_rows
    slot_count = (max_tiles + data_count - 1) // data_count
    tile_ends = jnp.cumsum(tile_counts)
    tile_firsts = tile_ends - tile_counts
    sample_ids = jnp.arange(data_count, dtype=jnp.int32)
    tiles_here = jnp.arange(tile_rows, dtype=jnp.int32) * data_count + data_index
    owners = jnp.sum((tile_ends[None, :] <= tiles_here[:, None]).astype(jnp.int32), axis=1)
    owner_first = jnp.sum(
        jnp.where(sample_ids[None, :] == owners[:, None], tile_firsts[None, :], 0), axis=1
    )
    slots = (tiles_here - owner_first) // data_count
    is_mine = sample_ids == data_index
    my_first = jnp.sum(jnp.where(is_mine, tile_firsts, 0))
    my_count = jnp.sum(jnp.where(is_mine, tile_counts, 0))
    tile_order = jnp.arange(max_tiles, dtype=jnp.int32)
    sources = (my_first + tile_order) % data_count
    slot_index = tile_order // data_count
    image_span = max_tiles * tile_tok

    pieces = tensor_pieces(vis_rows.reshape(token_count, merge_count, part_width))
    whole = jnp.zeros((token_count, merge_count, vision_width), vis_rows.dtype)
    for step, piece in enumerate(pieces):
        start = (tensor_index - step) % tensor_count * part_width
        whole = lax.dynamic_update_slice_in_dim(whole, piece, start, 2)
    normed_vis = layer_norm(whole.astype(jnp.float32), ln_gain, ln_bias).astype(jnp.bfloat16)
    feature = vision_width // data_count
    blocks = normed_vis.reshape(token_count, merge_count, data_count, feature)
    blocks = blocks.transpose(2, 0, 1, 3).reshape(data_count, token_count, merge_count * feature)
    blocks = exchange(blocks, data_count, None, 0)
    proj = proj_weight.transpose(1, 0, 2).reshape(merge_count * feature, part_model)
    partial = jnp.dot(
        blocks.reshape(data_count * token_count, merge_count * feature),
        proj,
        preferred_element_type=jnp.float32,
    ).astype(jnp.bfloat16)
    image_cols = reduce_blocks(
        partial.reshape(outer, inner, token_count, part_model), 1
    ).reshape(tile_rows, tile_tok, part_model)

    empty_slots = jnp.zeros((data_count, slot_count) + image_cols.shape[1:], jnp.bfloat16)
    routed = empty_slots.at[owners, slots].set(image_cols)
    received = exchange(routed, data_count, None, 3)
    arrived = received[sources, slot_index]
    arrived = arrived.reshape(image_span, part_model)
    start_row = image_offsets[0]
    sequence = text_rows[0]
    current = lax.dynamic_slice_in_dim(sequence, start_row, image_span, 0)
    is_image = jnp.repeat(tile_order < my_count, tile_tok)[:, None]
    combined = jnp.where(is_image, arrived, current)
    sequence = lax.dynamic_update_slice_in_dim(sequence, combined, start_row, 0)

    seq_len = sequence.shape[0]
    model_width = attn_gain.shape[0]
    seq_float = sequence.astype(jnp.float32)
    squares = lax.psum(jnp.sum(seq_float * seq_float, axis=-1), "tensor")[:, None]
    gain = lax.dynamic_slice_in_dim(attn_gain, tensor_index * part_model, part_model, 0)
    normalized = (
        seq_float * lax.rsqrt(squares / model_width + decoder_epsilon) * gain
    ).astype(jnp.bfloat16)
    held_rows = part_model // depth // inner
    normalized = normalized.reshape(seq_len, held_rows, inner, depth).transpose(2, 0, 1, 3)
    normalized = exchange(
        normalized.reshape(inner, seq_len, held_rows * depth), inner, True, 4
    )
    pieces = tensor_pieces(normalized)
    product = product_blocks(pieces, weight, 5)
    part_query = w_query.shape[1]
    context = attend(product, part_query)
    return context.reshape(1, seq_len, context.shape[1])


def solution(mesh):
    in_specs = (
        P(None, "dp", None, "tensor"),
        P(),
        P(),
        P("dp", None, "tensor"),
        P("dp", None, "tensor"),
        P(),
        P("dp", "tensor"),
        P("dp", None, "tensor"),
        P(),
        P("dp"),
    )
    out_specs = P("dp", None, "tensor")
    return jax.shard_map(
        per_device, mesh=mesh, in_specs=in_specs, out_specs=out_specs, check_vma=False
    )
```

profile of v0, /device:TPU:10, one launch (start us, length us, event | category | flops | bytes accessed | tf_op | source)
XLA Modules:
  0.0 521.0 jit_solution(9623340698188769713)
XLA Ops:
  6.5 4.1 copy.34
  10.9 1.9 pad_maximum_fusion
  12.8 2.0 copy.20
  14.8 3.9 copy.23
  19.7 0.7 fusion.17
  21.1 6.4 %dynamic_update_slice.9 = bf16[64,2,3200]{2,0,1:T(8,128)(2,1)S(1)} dynamic-update-slice(bf16[64,2,3200]{2,0,1:T(8,128)(2,1)S(1)} %broadcast_in_dim.60, bf16[64,2,1600]{2,0,1:T(8,128)(2,1)} %copy.20, s32[]{:T(128)} %constant.85.clone.1, s32[]{:T(128)} %constant.85.clone.1, s32[]{:T(128)S(6)} %select_n.122) | dynamic-update-slice | bytes 819204 | tf_op jit(solution)/shard_map/dynamic_update_slice | solution.py:415
  28.6 6.7 %dynamic_update_slice.10 = bf16[64,2,3200]{2,0,1:T(8,128)(2,1)S(1)} dynamic-update-slice(bf16[64,2,3200]{2,0,1:T(8,128)(2,1)S(1)} %dynamic_update_slice.9, bf16[64,2,1600]{2,0,1:T(8,128)(2,1)} %collective-permute-done, s32[]{:T(128)} %constant.85.clone.1, s32[]{:T(128)} %constant.85.clone.1, s32[]{:T(128)S(6)} %select_n.124) | dynamic-update-slice | bytes 819204 | tf_op jit(solution)/shard_map/dynamic_update_slice | solution.py:415
  36.4 3.1 reshape.269
  39.5 1.1 copy.22
  40.6 0.6 reshape.270.x_ref
  41.3 51.9 %shard_map.100 = bf16[16,64,400]{2,1,0:T(8,128)(2,1)S(1)} custom-call(bf16[16,64,400]{2,1,0:T(8,128)(2,1)S(1)} %reshape.270.x_ref), custom_call_target="tpu_custom_call" | custom-call | bytes 16384000 | tf_op jit(solution)/shard_map/pallas_call | solution.py:282
  93.1 6.7 %convolution_convert_fusion = bf16[1024,4096]{1,0:T(8,128)(2,1)S(1)} fusion(bf16[1024,400]{1,0:T(8,128)(2,1)S(1)} %bitcast.46, bf16[400,4096]{1,0:T(8,128)(2,1)} %bitcast.51), kind=kOutput, calls=%fused_computation.4 | convolution fusion | flops 3359637504 | bytes 12484608 | tf_op jit(solution)/shard_map/dot_general | solution.py:422
  99.8 141.7 %shard_map.101 = bf16[64,4096]{1,0:T(8,128)(2,1)S(1)} custom-call(bf16[4,4,64,4096]{3,2,1,0:T(8,128)(2,1)S(1)} %bitcast.43), custom_call_target="tpu_custom_call" | custom-call | bytes 251658240 | tf_op jit(solution)/shard_map/pallas_call | solution.py:168
  241.6 0.8 scatter_fusion
  242.4 53.5 %shard_map.102 = bf16[16,1,8,4096]{3,2,1,0:T(8,128)(2,1)S(1)} custom-call(bf16[16,1,8,4096]{3,2,1,0:T(8,128)(2,1)S(1)} %bitcast.44), custom_call_target="tpu_custom_call" | custom-call | bytes 20971520 | tf_op jit(solution)/shard_map/pallas_call | solution.py:282
  295.9 1.6 gather_fusion
  297.5 3.2 bitcast_select_fusion
  300.7 6.9 %dynamic_update_slice.11 = bf16[384,4096]{1,0:T(8,128)(2,1)S(1)} dynamic-update-slice(bf16[384,4096]{1,0:T(8,128)(2,1)S(1)} %bitcast.47, bf16[128,4096]{1,0:T(8,128)(2,1)} %bitcast_select_fusion, s32[]{:T(128)S(6)} %select_n.130, s32[]{:T(128)} %constant.85.clone.1) | dynamic-update-slice | bytes 2097156 | tf_op jit(solution)/shard_map/dynamic_update_slice | solution.py:441
  307.6 0.7 fusion
  308.3 2.5 psum.7
  310.8 2.7 fusion.2
  313.4 4.8 reshape.276
  318.2 4.1 copy.27
  322.3 4.7 reshape.277.x_ref
  327.0 40.5 %shard_map.103.refs_0_ = bf16[4,384,1024]{2,1,0:T(8,128)(2,1)S(1)} custom-call(bf16[4,384,1024]{2,1,0:T(8,128)(2,1)S(1)} %reshape.277.x_ref), custom_call_target="tpu_custom_call" | custom-call | bytes 62914560 | tf_op jit(solution)/shard_map/pallas_call | solution.py:282
  367.5 1.7 copy-done.1
  369.2 0.7 fusion.11
  370.1 4.7 collective-permute-done.1.refs_1_
  374.9 1.7 copy-done.9
  376.5 126.4 %shard_map.104.q_ref.k_ref.v_ref = f32[384,3072]{1,0:T(8,128)} custom-call(bf16[4,384,1024]{2,1,0:T(8,128)(2,1)} %copy-done.1, bf16[4,384,1024]{2,1,0:T(8,128)(2,1)} %copy-done.9, bf16[2048,3072]{1,0:T(8,128)(2,1)} %all-gather.2.cloned.1.call-done.refs_2_), custom_call_target="tpu_custom_call" | custom-call | flops 19327352832 | bytes 209715200 | tf_op jit(solution)/shard_map/pallas_call | solution.py:256
  502.9 2.3 copy-done
  505.3 8.9 %shard_map.105 = bf16[384,2048]{1,0:T(8,128)(2,1)} custom-call(f32[384,3072]{1,0:T(8,128)S(1)} %copy-done, f32[384,3072]{1,0:T(8,128)S(1)} %copy-done, f32[384,3072]{1,0:T(8,128)S(1)} %copy-done, f32[384,128]{1,0:T(8,128)S(1)} %get-tuple-element.11.cos_ref, f32[384,128]{1,0:T(8,128)S(1)} %get-tuple-element.12.sin_ref), custom_call_target="tpu_custom_call" | custom-call | tf_op jit(solution)/shard_map/pallas_call | solution.py:349
  (47 shorter events, 3.7 us)
Async XLA Ops:
  6.5 4.3 copy-start.4
  6.5 4.1 copy-start.5
  6.5 368.3 %all-gather.2.cloned.1.call-start = ((), (), s32[]{:S(2)}) async-start(), calls=%async_computation | async-start | bytes 15728640 | tf_op jit(solution)/shard_map/all_gather | solution.py:390
  12.8 2.1 copy-start.3
  14.8 13.8 %collective-permute-start = (bf16[64,2,1600]{2,0,1:T(8,128)(2,1)}, bf16[64,2,1600]{2,0,1:T(8,128)(2,1)}, u32[]{:S(2)}, u32[]{:S(2)}) collective-permute-start(bf16[64,2,1600]{2,0,1:T(8,128)(2,1)} %copy.20), channel_id=1, source_target_pairs={{0,1},{1,0},{2,3},{3,2},{4,5},{5,4},{6,7},{7,6},{8,9},{9,8},{10,11... | collective-permute-start | bytes 1228808 | tf_op jit(solution)/shard_map/ppermute | solution.py:306
  14.8 3.9 copy-start.8
  18.8 17.2 %copy-start.6 = (f32[2,3200]{1,0:T(2,128)S(1)}, f32[2,3200]{1,0:T(2,128)}, u32[]{:S(2)}) copy-start(f32[2,3200]{1,0:T(2,128)} %param.12) | copy-start | bytes 76804
  18.8 17.2 %copy-start.7 = (f32[2,3200]{1,0:T(2,128)S(1)}, f32[2,3200]{1,0:T(2,128)}, u32[]{:S(2)}) copy-start(f32[2,3200]{1,0:T(2,128)} %param.11) | copy-start | bytes 76804
  297.5 3.2 copy-start.2
  300.7 10.0 %dynamic-slice-start = ((f32[8192]{0:T(1024)}, s32[]{:T(128)}), f32[4096]{0:T(1024)S(1)}, s32[]{:S(2)}) async-start(f32[8192]{0:T(1024)} %param.15, s32[]{:T(128)} %select_n.132), calls=%async_computation.1 | async-start | bytes 33280 | tf_op jit(solution)/shard_map/dynamic_slice | solution.py:447
  367.5 1.7 copy-start.1
  369.2 5.7 %collective-permute-start.1 = (bf16[4,384,1024]{2,1,0:T(8,128)(2,1)S(1)}, bf16[4,384,1024]{2,1,0:T(8,128)(2,1)S(1)}, u32[]{:S(2)}, u32[]{:S(2)}) collective-permute-start(bf16[4,384,1024]{2,1,0:T(8,128)(2,1)S(1)} %shard_map.103.refs_0_), channel_id=1, source_target_pairs={{0,1},{1,0},{2,3},{3,2},{4,5},{5,4},{6,7},{7,6},{8,9},{9,8},{10,11... | collective-permute-start | bytes 9437192 | tf_op jit(solution)/shard_map/ppermute | solution.py:306
  374.9 1.7 copy-start.9
  502.9 2.3 copy-start
Sparse Core Ops, SparseCore 0:
  12.9 304.9 all-gather.1
where the time goes:
time: 522 us; the launch traced here: 521 us
  Pallas kernels  423 us (81%)
  local copies, waits for them, and re-layouts  57.1 us (11%)
  between operations  14.3 us (3%)
  other arithmetic  12.9 us (2%)
  matrix products  6.66 us (1%)
    pallas_call x3, Pallas kernels, exchange(): pl.pallas_call(functools.partial(exchange_kernel, size, inner, plane), ou...  146 us
    pallas_call x1, Pallas kernels, reduce_blocks(): pl.pallas_call(functools.partial(reduce_kernel, inner, chunks, math.gcd(t...  142 us
    pallas_call x1, Pallas kernels, product_blocks(): pl.pallas_call(functools.partial(product_kernel, inner, count, math.gcd(c...  126 us
    unnamed x23, local copies, waits for them, and re-layouts  14 us
    dynamic_update_slice x2, local copies, waits for them, and re-layouts, per_device(): whole = lax.dynamic_update_slice_in_dim(whole, piece, start, 2)  13.1 us
  transfers between devices with their start and end apart: 3, of which 1 were waited for; matrix products, arithmetic and copies ran while one was open for 12% of the time, Pallas kernels for 55%

commit v1 on v0

v1 whole, which is shorter than its diff:
```python
import functools
import math

import jax
import jax.numpy as jnp
from jax import lax
from jax.experimental import pallas as pl
from jax.experimental.pallas import tpu as pltpu
from jax.sharding import PartitionSpec as P

QUERY_HEADS = 32
KEY_VALUE_HEADS = 8
HEAD_WIDTH = 128


vision_epsilon = 1e-06
decoder_epsilon = 1e-05
rope_base = 500000.0

MESH = pl.DeviceIdType.MESH
NEAR = 4


def near_of(index, mid):
    return index // (2 * mid) % 2 * 2 + index % 2


def far_of(index, mid):
    return index // (4 * mid) * mid + index // 2 % mid


def join(near, far, mid):
    return (far // mid * 2 + near // 2) * (2 * mid) + far % mid * 2 + near % 2


def middle(data_count, tensor_count):
    spare = int(math.log2(data_count)) - int(math.log2(tensor_count)) - 1
    return 1 << (min(2, spare) - 1)


def here(mid):
    data_index = lax.axis_index("dp")
    return near_of(data_index, mid), far_of(data_index, mid), lax.axis_index("tensor")


def meet(mid, near=True, far=True, twin=True):
    me, my_far, tensor_index = here(mid)
    far_count = lax.axis_size("dp") // NEAR
    tensor_count = lax.axis_size("tensor")
    targets = []
    if near:
        targets += [{"dp": join((me + s) % NEAR, my_far, mid)} for s in range(1, NEAR)]
    if far:
        targets += [{"dp": join(me, (my_far + s) % far_count, mid)} for s in range(1, far_count)]
    if twin:
        targets += [{"tensor": (tensor_index + s) % tensor_count} for s in range(1, tensor_count)]
    barrier = pltpu.get_barrier_semaphore()
    for target in targets:
        pl.semaphore_signal(barrier, inc=1, device_id=target, device_id_type=MESH)
    pl.semaphore_wait(barrier, len(targets))


def remote(src_ref, dst_ref, send_sem, recv_sem, device):
    return pltpu.make_async_remote_copy(
        src_ref=src_ref,
        dst_ref=dst_ref,
        send_sem=send_sem,
        recv_sem=recv_sem,
        device_id=device,
        device_id_type=MESH,
    )


def front_kernel(mid, x_ref, gain_ref, bias_ref, pw_ref, pwg_ref, vg_ref, normed, stat_out,
                 stat_in, pw_send, pw_recv, st_send, st_recv, far_send, far_recv, near_send,
                 near_recv, twin_send, twin_recv):
    blocks, tokens, width = x_ref.shape
    far_count = vg_ref.shape[1]
    rows, wide = pwg_ref.shape[1:]
    tensor_count = lax.axis_size("tensor")
    me, my_far, tensor_index = here(mid)
    meet(mid)
    pw_copies = []
    for step in range(1, NEAR):
        target = (me + step) % NEAR
        copy = remote(
            pw_ref.at[:, pl.ds(pl.multiple_of(target * wide, wide), wide)],
            pwg_ref.at[me],
            pw_send.at[step - 1],
            pw_recv.at[step - 1],
            {"dp": join(target, my_far, mid)},
        )
        copy.start()
        pw_copies.append(copy)

    count = blocks * width
    total = jnp.zeros((tokens, 1), jnp.float32)
    for at in range(blocks):
        total = total + jnp.sum(x_ref[at].astype(jnp.float32), axis=-1, keepdims=True)
    mean = total / count
    spread = jnp.zeros((tokens, 1), jnp.float32)
    for at in range(blocks):
        centered = x_ref[at].astype(jnp.float32) - mean
        spread = spread + jnp.sum(centered * centered, axis=-1, keepdims=True)
    stat_out[0] = jnp.broadcast_to(mean, stat_out.shape[1:])
    stat_out[1] = jnp.broadcast_to(spread, stat_out.shape[1:])
    stat_copies = []
    for step in range(1, tensor_count):
        copy = remote(
            stat_out,
            stat_in.at[step - 1],
            st_send.at[step - 1],
            st_recv.at[step - 1],
            {"tensor": (tensor_index + step) % tensor_count},
        )
        copy.start()
        stat_copies.append(copy)
    for copy in stat_copies:
        copy.wait_recv()
    means, spreads = [mean], [spread]
    for step in range(1, tensor_count):
        means.append(stat_in[step - 1, 0][:, :1])
        spreads.append(stat_in[step - 1, 1][:, :1])
    average = sum(means) / tensor_count
    variance = sum(s + count * (one - average) * (one - average) for s, one in zip(spreads, means))
    scale = lax.rsqrt(variance / (count * tensor_count) + vision_epsilon)
    far_copies = []
    for at in range(blocks):
        centered = (x_ref[at].astype(jnp.float32) - average) * scale
        normed[at] = (centered * gain_ref[pl.ds(at, 1)] + bias_ref[pl.ds(at, 1)]).astype(
            normed.dtype
        )
        goal = tensor_index * blocks + at
        mine = goal == my_far
        copy = remote(
            normed.at[at],
            vg_ref.at[me, my_far],
            far_send.at[at],
            far_recv.at[my_far],
            {"dp": join(me, goal, mid)},
        )
        pl.when(jnp.logical_not(mine))(copy.start)
        far_copies.append((mine, copy))

        @pl.when(mine)
        def _():
            vg_ref[me, my_far] = normed[at]

    holder = my_far // blocks == tensor_index

    def twin_copy(ahead, step, block):
        return remote(
            vg_ref.at[block],
            vg_ref.at[block],
            twin_send.at[ahead - 1, step],
            twin_recv.at[step],
            {"tensor": (tensor_index + ahead) % tensor_count},
        )

    @pl.when(holder)
    def _():
        for step in range(1, far_count):
            source = (my_far + step) % far_count
            remote(
                normed.at[0],
                vg_ref.at[me, source],
                far_send.at[0],
                far_recv.at[source],
                {"dp": join(me, source, mid)},
            ).wait_recv()
        near_copies, twin_copies = [], []
        for step in range(1, NEAR):
            copy = remote(
                vg_ref.at[me],
                vg_ref.at[me],
                near_send.at[step - 1],
                near_recv.at[step - 1],
                {"dp": join((me + step) % NEAR, my_far, mid)},
            )
            copy.start()
            near_copies.append(copy)
        for step in range(NEAR):
            block = (me + NEAR - step) % NEAR
            if step:
                remote(
                    vg_ref.at[me],
                    vg_ref.at[block],
                    near_send.at[step - 1],
                    near_recv.at[step - 1],
                    {"dp": join(block, my_far, mid)},
                ).wait_recv()
            for ahead in range(1, tensor_count):
                copy = twin_copy(ahead, step, block)
                copy.start()
                twin_copies.append(copy)
        for copy in near_copies + twin_copies:
            copy.wait_send()

    def keep(at, carry):
        window = pl.ds(pl.multiple_of(at * 16, 16), 16)
        pwg_ref[me, window] = pw_ref[window, pl.ds(pl.multiple_of(me * wide, wide), wide)]
        return carry

    lax.fori_loop(0, rows // 16, keep, 0)

    @pl.when(jnp.logical_not(holder))
    def _():
        for step in range(NEAR):
            twin_copy(1, step, (me + NEAR - step) % NEAR).wait_recv()

    for mine, copy in far_copies:
        pl.when(jnp.logical_not(mine))(copy.wait_send)
    for copy in stat_copies:
        copy.wait_send()
    for copy in pw_copies:
        copy.wait()


def front(x, gain, bias, proj, data_count, tensor_count, mid):
    blocks, tokens, width = x.shape
    far_count = data_count // NEAR
    rows, columns = proj.shape
    vmem = pl.BlockSpec(memory_space=pltpu.VMEM)
    dma = pltpu.SemaphoreType.DMA
    return pl.pallas_call(
        functools.partial(front_kernel, mid),
        out_shape=(
            jax.ShapeDtypeStruct((NEAR, rows, columns // NEAR), proj.dtype),
            jax.ShapeDtypeStruct((NEAR, far_count, tokens, width), x.dtype),
        ),
        in_specs=[vmem] * 4,
        out_specs=(vmem, vmem),
        scratch_shapes=[
            pltpu.VMEM((blocks, tokens, width), x.dtype),
            pltpu.VMEM((2, tokens, 128), jnp.float32),
            pltpu.VMEM((tensor_count - 1, 2, tokens, 128), jnp.float32),
            dma((NEAR - 1,)),
            dma((NEAR - 1,)),
            dma((tensor_count - 1,)),
            dma((tensor_count - 1,)),
            dma((blocks,)),
            dma((far_count,)),
            dma((NEAR - 1,)),
            dma((NEAR - 1,)),
            dma((tensor_count - 1, NEAR)),
            dma((NEAR,)),
        ],
        compiler_params=pltpu.CompilerParams(
            collective_id=0, has_side_effects=True, vmem_limit_bytes=40 << 20
        ),
        cost_estimate=pl.CostEstimate(flops=0, bytes_accessed=80 << 20, transcendentals=0),
    )(x, gain, bias, proj)


def far_order(far_count):
    half = far_count // 2
    return [half] + [s for s in range(1, far_count) if s != half]


def project_kernel(mid, tile, rows, vg_ref, pw_ref, o_ref, total, leaving, held, send, recv):
    near, far_count, tokens, width = vg_ref.shape
    me, my_far, _ = here(mid)
    columns = o_ref.shape[1]

    def compute(block, dst_ref):
        def one(at, carry):
            part = pl.ds(pl.multiple_of(at * tile, tile), tile)
            term = jnp.dot(
                vg_ref[:, block].reshape(near * tokens, width),
                pw_ref[:, part],
                preferred_element_type=jnp.float32,
            )
            dst_ref[:, part] = term.astype(dst_ref.dtype)
            return carry

        lax.fori_loop(0, columns // tile, one, 0)

    meet(mid, near=False, twin=False)
    copies = []
    for step in far_order(far_count):
        target = (my_far + step) % far_count
        compute(target, leaving.at[step - 1])
        copy = remote(
            leaving.at[step - 1],
            held.at[step - 1],
            send.at[step - 1],
            recv.at[step - 1],
            {"dp": join(me, target, mid)},
        )
        copy.start()
        copies.append(copy)
    compute(my_far, total)
    for copy in copies:
        copy.wait_recv()

    def add(at, carry):
        window = pl.ds(pl.multiple_of(at * rows, rows), rows)
        value = total[window, :]
        for step in range(1, far_count):
            value = value + held[step - 1, window, :].astype(jnp.float32)
        o_ref[window, :] = value.astype(o_ref.dtype)
        return carry

    lax.fori_loop(0, o_ref.shape[0] // rows, add, 0)
    for copy in copies:
        copy.wait_send()


def project(vg, pw, mid):
    near, far_count, tokens, width = vg.shape
    columns = pw.shape[1]
    shape = (near * tokens, columns)
    dma = pltpu.SemaphoreType.DMA
    return pl.pallas_call(
        functools.partial(project_kernel, mid, math.gcd(columns, 512), 16),
        out_shape=jax.ShapeDtypeStruct(shape, vg.dtype),
        in_specs=[pl.BlockSpec(memory_space=pltpu.VMEM)] * 2,
        out_specs=pl.BlockSpec(memory_space=pltpu.VMEM),
        scratch_shapes=[
            pltpu.VMEM(shape, jnp.float32),
            pltpu.VMEM((far_count - 1,) + shape, vg.dtype),
            pltpu.VMEM((far_count - 1,) + shape, vg.dtype),
            dma((far_count - 1,)),
            dma((far_count - 1,)),
        ],
        compiler_params=pltpu.CompilerParams(
            collective_id=1, has_side_effects=True, vmem_limit_bytes=40 << 20
        ),
        cost_estimate=pl.CostEstimate(
            flops=2 * far_count * near * tokens * width * columns,
            bytes_accessed=80 << 20,
            transcendentals=0,
        ),
    )(vg, pw)


def route_kernel(mid, x_ref, o_ref, send, recv, own_sem):
    size = x_ref.shape[0]
    data_index = lax.axis_index("dp")
    me, my_far, _ = here(mid)
    own = pltpu.make_async_copy(x_ref.at[data_index], o_ref.at[me, my_far], own_sem)
    own.start()
    barrier = pltpu.get_barrier_semaphore()
    for step in range(1, size):
        pl.semaphore_signal(
            barrier,
            inc=1,
            device_id={"dp": (data_index + step) % size},
            device_id_type=MESH,
        )
    pl.semaphore_wait(barrier, size - 1)
    copies = []
    for step in range(1, size):
        target = (data_index + step) % size
        copy = remote(
            x_ref.at[target],
            o_ref.at[me, my_far],
            send.at[step - 1],
            recv.at[step - 1],
            {"dp": target},
        )
        copy.start()
        copies.append(copy)
    own.wait()
    for copy in copies:
        copy.wait()


def route(tiles, mid):
    size = tiles.shape[0]
    dma = pltpu.SemaphoreType.DMA
    return pl.pallas_call(
        functools.partial(route_kernel, mid),
        out_shape=jax.ShapeDtypeStruct((NEAR, size // NEAR) + tiles.shape[1:], tiles.dtype),
        in_specs=[pl.BlockSpec(memory_space=pltpu.VMEM)],
        out_specs=pl.BlockSpec(memory_space=pltpu.VMEM),
        scratch_shapes=[dma((size - 1,)), dma((size - 1,)), dma],
        compiler_params=pltpu.CompilerParams(
            collective_id=2, has_side_effects=True, vmem_limit_bytes=24 << 20
        ),
        cost_estimate=pl.CostEstimate(flops=0, bytes_accessed=40 << 20, transcendentals=0),
    )(tiles)


def sequence_kernel(mid, rows, spot_ref, text_ref, got_ref, gain_ref, a_ref, seq, sums, sums_in,
                    leaving, st_send, st_recv, near_send, near_recv, twin_send, twin_recv):
    tensor_count, _, seq_len, held = a_ref.shape
    near, _, wide = got_ref.shape
    model_width = text_ref.shape[1] * tensor_count
    me, my_far, tensor_index = here(mid)
    shift = held // (lax.axis_size("dp") // NEAR // tensor_count)
    meet(mid, far=False)

    def fill(at, carry):
        window = pl.ds(pl.multiple_of(at * rows, rows), rows)
        place = lax.broadcasted_iota(jnp.int32, (rows, spot_ref.shape[1]), 0) + at * rows
        chosen = jnp.where(place == spot_ref[...], 1.0, 0.0)
        image = jnp.max(chosen, axis=-1, keepdims=True) > 0.5
        chosen = chosen.astype(jnp.bfloat16)
        squares = jnp.zeros((rows, 1), jnp.float32)
        for part in range(near):
            lanes = pl.ds(part * wide, wide)
            drawn = jnp.dot(chosen, got_ref[part], preferred_element_type=jnp.float32)
            value = jnp.where(image, drawn, text_ref[window, lanes].astype(jnp.float32))
            seq[window, lanes] = value.astype(seq.dtype)
            squares = squares + jnp.sum(value * value, axis=-1, keepdims=True)
        sums[window, :] = jnp.broadcast_to(squares, (rows, sums.shape[1]))
        return carry

    lax.fori_loop(0, seq_len // rows, fill, 0)
    stat_copies = []
    for step in range(1, tensor_count):
        copy = remote(
            sums,
            sums_in.at[step - 1],
            st_send.at[step - 1],
            st_recv.at[step - 1],
            {"tensor": (tensor_index + step) % tensor_count},
        )
        copy.start()
        stat_copies.append(copy)
    for copy in stat_copies:
        copy.wait_recv()

    def norm(target, store):
        def one(at, carry):
            window = pl.ds(pl.multiple_of(at * rows, rows), rows)
            squares = sums[window, :][:, :1]
            for step in range(1, tensor_count):
                squares = squares + sums_in[step - 1, window, :][:, :1]
            scale = lax.rsqrt(squares / model_width + decoder_epsilon)
            for part in range(held // shift):
                lanes = pl.ds(pl.multiple_of(join(target, part, mid) * shift, shift), shift)
                value = seq[window, lanes].astype(jnp.float32) * scale * gain_ref[:, lanes]
                store(window, pl.ds(part * shift, shift), value.astype(jnp.bfloat16))
            return carry

        lax.fori_loop(0, seq_len // rows, one, 0)

    near_copies, twin_copies = [], []
    for step in range(1, NEAR):
        target = (me + step) % NEAR

        def leave(window, lanes, value):
            leaving[step - 1, window, lanes] = value

        norm(target, leave)
        copy = remote(
            leaving.at[step - 1],
            a_ref.at[tensor_index, me],
            near_send.at[step - 1],
            near_recv.at[step - 1],
            {"dp": join(target, my_far, mid)},
        )
        copy.start()
        near_copies.append(copy)

    def stay(window, lanes, value):
        a_ref[tensor_index, me, window, lanes] = value

    norm(me, stay)

    def twin_copy(ahead, step, owner):
        block = (me + NEAR - step) % NEAR
        return remote(
            a_ref.at[owner, block],
            a_ref.at[owner, block],
            twin_send.at[ahead - 1, step],
            twin_recv.at[ahead - 1, step],
            {"tensor": (tensor_index + ahead) % tensor_count},
        )

    for step in range(NEAR):
        if step:
            remote(
                leaving.at[step - 1],
                a_ref.at[tensor_index, (me + NEAR - step) % NEAR],
                near_send.at[step - 1],
                near_recv.at[step - 1],
                {"dp": join((me + step) % NEAR, my_far, mid)},
            ).wait_recv()
        for ahead in range(1, tensor_count):
            copy = twin_copy(ahead, step, tensor_index)
            copy.start()
            twin_copies.append(copy)
    for ahead in range(1, tensor_count):
        for step in range(NEAR):
            owner = (tensor_index + tensor_count - ahead) % tensor_count
            twin_copy(ahead, step, owner).wait_recv()
    for copy in near_copies + twin_copies + stat_copies:
        copy.wait_send()


def sequences(spots, text, got, gain, data_count, tensor_count, mid):
    seq_len, part_model = text.shape
    held = part_model // NEAR
    vmem = pl.BlockSpec(memory_space=pltpu.VMEM)
    dma = pltpu.SemaphoreType.DMA
    return pl.pallas_call(
        functools.partial(sequence_kernel, mid, math.gcd(seq_len, 32)),
        out_shape=jax.ShapeDtypeStruct((tensor_count, NEAR, seq_len, held), text.dtype),
        in_specs=[vmem] * 4,
        out_specs=vmem,
        scratch_shapes=[
            pltpu.VMEM((seq_len, part_model), text.dtype),
            pltpu.VMEM((seq_len, 128), jnp.float32),
            pltpu.VMEM((tensor_count - 1, seq_len, 128), jnp.float32),
            pltpu.VMEM((NEAR - 1, seq_len, held), text.dtype),
            dma((tensor_count - 1,)),
            dma((tensor_count - 1,)),
            dma((NEAR - 1,)),
            dma((NEAR - 1,)),
            dma((tensor_count - 1, NEAR)),
            dma((tensor_count - 1, NEAR)),
        ],
        compiler_params=pltpu.CompilerParams(
            collective_id=3, has_side_effects=True, vmem_limit_bytes=40 << 20
        ),
        cost_estimate=pl.CostEstimate(flops=0, bytes_accessed=100 << 20, transcendentals=0),
    )(spots, text, got, gain)


def product_kernel(mid, tile, rows, a_ref, w_ref, o_ref, leaving, held, send_sem, recv_sem):
    count, _, seq_len, depth = a_ref.shape
    me, my_far, _ = here(mid)
    tiles = o_ref.shape[1] // tile

    def compute(block, dst_ref, low, high):
        def one(at, carry):
            part = pl.ds(pl.multiple_of(at * tile, tile), tile)
            total = None
            for piece in range(count):
                term = jnp.dot(
                    a_ref[piece, block],
                    w_ref[pl.ds(piece * depth, depth), part],
                    preferred_element_type=jnp.float32,
                )
                total = term if total is None else total + term
            dst_ref[:, part] = total.astype(dst_ref.dtype)
            return carry

        lax.fori_loop(low, high, one, 0)

    meet(mid, far=False, twin=False)
    copies = []
    for step in range(1, NEAR + 1):
        block = (me + step) % NEAR
        dst_ref = leaving.at[step - 1] if step < NEAR else o_ref
        compute(block, dst_ref, 0, 1)
        if copies:
            copies[-1].start()
        compute(block, dst_ref, 1, tiles)
        if step < NEAR:
            copies.append(
                remote(
                    leaving.at[step - 1],
                    held.at[step - 1],
                    send_sem.at[step - 1],
                    recv_sem.at[step - 1],
                    {"dp": join(block, my_far, mid)},
                )
            )
    for copy in copies:
        copy.wait_recv()

    def add(at, carry):
        window = pl.ds(pl.multiple_of(at * rows, rows), rows)
        total = o_ref[window, :]
        for step in range(1, NEAR):
            total = total + held[step - 1, window, :].astype(jnp.float32)
        o_ref[window, :] = total
        return carry

    lax.fori_loop(0, seq_len // rows, add, 0)
    for copy in copies:
        copy.wait_send()


def product_blocks(a, weight, mid):
    count, _, seq_len, depth = a.shape
    columns = weight.shape[1]
    return pl.pallas_call(
        functools.partial(product_kernel, mid, math.gcd(columns, 512), math.gcd(seq_len, 16)),
        out_shape=jax.ShapeDtypeStruct((seq_len, columns), jnp.float32),
        in_specs=[pl.BlockSpec(memory_space=pltpu.VMEM)] * 2,
        out_specs=pl.BlockSpec(memory_space=pltpu.VMEM),
        scratch_shapes=[
            pltpu.VMEM((NEAR - 1, seq_len, columns), jnp.bfloat16),
            pltpu.VMEM((NEAR - 1, seq_len, columns), jnp.bfloat16),
            pltpu.SemaphoreType.DMA((NEAR - 1,)),
            pltpu.SemaphoreType.DMA((NEAR - 1,)),
        ],
        compiler_params=pltpu.CompilerParams(
            collective_id=4, has_side_effects=True, vmem_limit_bytes=56 << 20
        ),
        cost_estimate=pl.CostEstimate(
            flops=2 * count * NEAR * seq_len * depth * columns,
            bytes_accessed=200 << 20,
            transcendentals=0,
        ),
    )(a, weight)


def attend_kernel(group, q_ref, k_ref, v_ref, cos_ref, sin_ref, o_ref):
    cosine, sine = cos_ref[...], sin_ref[...]

    def turn(rows):
        return (rows * cosine + pltpu.roll(rows, HEAD_WIDTH // 2, 1) * sine).astype(jnp.bfloat16)

    key_rows = turn(k_ref[...])
    value_rows = v_ref[...].astype(jnp.bfloat16)
    seq_len = key_rows.shape[0]
    row_at = lax.broadcasted_iota(jnp.int32, (seq_len, seq_len), 0)
    column_at = lax.broadcasted_iota(jnp.int32, (seq_len, seq_len), 1)
    for head in range(group):
        part = pl.ds(head * HEAD_WIDTH, HEAD_WIDTH)
        query_rows = turn(q_ref[:, part])
        scores = lax.dot_general(
            query_rows, key_rows, (((1,), (1,)), ((), ())), preferred_element_type=jnp.float32
        ) * HEAD_WIDTH ** (-0.5)
        scores = jnp.where(row_at >= column_at, scores, -1e30)
        exponentials = jnp.exp(scores - jnp.max(scores, axis=-1, keepdims=True))
        weights = exponentials / jnp.sum(exponentials, axis=-1, keepdims=True)
        context = jnp.dot(
            weights.astype(jnp.bfloat16), value_rows, preferred_element_type=jnp.float32
        )
        o_ref[:, part] = context.astype(o_ref.dtype)


def attend(product, part_query):
    seq_len, columns = product.shape
    group = QUERY_HEADS // KEY_VALUE_HEADS
    local_kv = part_query // HEAD_WIDTH // group
    key_at = part_query // HEAD_WIDTH
    half_width = HEAD_WIDTH // 2
    exponents = jnp.arange(half_width, dtype=jnp.float32) * (2.0 / HEAD_WIDTH)
    frequency = rope_base ** (-exponents)
    angles = jnp.arange(seq_len, dtype=jnp.float32)[:, None] * frequency[None, :]
    cosine, sine = jnp.cos(angles), jnp.sin(angles)
    cosine = jnp.concatenate([cosine, cosine], axis=1)
    sine = jnp.concatenate([-sine, sine], axis=1)
    table = pl.BlockSpec((seq_len, HEAD_WIDTH), lambda g: (0, 0))
    return pl.pallas_call(
        functools.partial(attend_kernel, group),
        grid=(local_kv,),
        out_shape=jax.ShapeDtypeStruct((seq_len, part_query), jnp.bfloat16),
        in_specs=[
            pl.BlockSpec((seq_len, group * HEAD_WIDTH), lambda g: (0, g)),
            pl.BlockSpec((seq_len, HEAD_WIDTH), lambda g: (0, key_at + g)),
            pl.BlockSpec((seq_len, HEAD_WIDTH), lambda g: (0, key_at + local_kv + g)),
            table,
            table,
        ],
        out_specs=pl.BlockSpec((seq_len, group * HEAD_WIDTH), lambda g: (0, g)),
        compiler_params=pltpu.CompilerParams(vmem_limit_bytes=24 << 20),
    )(product, product, product, cosine, sine)


def per_device(
    vis_rows,
    ln_gain,
    ln_bias,
    proj_weight,
    text_rows,
    attn_gain,
    w_query,
    key_value_weight,
    tile_counts,
    image_offsets,
):
    data_count = lax.axis_size("dp")
    data_index = lax.axis_index("dp")
    tensor_count = lax.axis_size("tensor")
    tensor_index = lax.axis_index("tensor")
    tile_rows, tile_tok, merge_count, part_width = vis_rows.shape
    feature = proj_weight.shape[0]
    part_model = proj_weight.shape[2]
    tokens = tile_rows * tile_tok
    mid = middle(data_count, tensor_count)
    far_count = data_count // NEAR
    far_here = far_count // tensor_count
    depth = w_query.shape[0]
    groups = [[join(p, f, mid) for f in range(far_count)] for p in range(NEAR)]
    weight = jnp.concatenate([w_query, key_value_weight.reshape(depth, -1)], axis=1)
    weight = lax.all_gather(weight, "dp", axis=0, tiled=True, axis_index_groups=groups)

    tops = far_here // mid
    split = (tops, 2, mid, 2, feature)

    def arranged(rows):
        parts = rows.reshape(rows.shape[:-1] + split)
        lead = rows.ndim - 2
        order = (lead + 1, lead + 3) + tuple(range(lead)) + (lead + 2, lead + 4, lead, lead + 5)
        return parts.transpose(order).reshape((far_here,) + rows.shape[:lead] + (-1,))

    start = tensor_index * part_width
    gain = arranged(lax.dynamic_slice_in_dim(ln_gain, start, part_width, 1))
    bias = arranged(lax.dynamic_slice_in_dim(ln_bias, start, part_width, 1))
    rows_in = arranged(vis_rows.reshape(tokens, merge_count, part_width))
    proj = proj_weight.transpose(1, 0, 2).reshape(merge_count * feature, part_model)
    proj, normed = front(rows_in, gain, bias, proj, data_count, tensor_count, mid)
    image = project(normed, proj.reshape(-1, proj.shape[2]), mid)

    max_tiles = 2 * tile_rows
    tile_ends = jnp.cumsum(tile_counts)
    tile_firsts = tile_ends - tile_counts
    far_index = far_of(data_index, mid)
    sources = join(jnp.arange(NEAR, dtype=jnp.int32), far_index, mid)
    ranks = (sources[None, :] - tile_firsts[:, None]) % data_count
    taken = jnp.clip((tile_firsts[:, None] + ranks) // data_count, 0, tile_rows - 1)
    taken = taken + jnp.arange(NEAR, dtype=jnp.int32)[None, :] * tile_rows
    image = image.reshape(NEAR * tile_rows, tile_tok, image.shape[1])
    routed = image[taken].reshape(data_count, NEAR * tile_tok, image.shape[2])
    received = route(routed, mid).reshape(NEAR, data_count * tile_tok, image.shape[2])

    is_mine = jnp.arange(data_count, dtype=jnp.int32) == data_index
    my_first = jnp.sum(jnp.where(is_mine, tile_firsts, 0))
    my_count = jnp.sum(jnp.where(is_mine, tile_counts, 0))
    far_ids = jnp.arange(far_count, dtype=jnp.int32)[:, None]
    tile_ids = join(jnp.arange(NEAR, dtype=jnp.int32)[None, :], far_ids, mid).reshape(-1)
    order = (tile_ids - my_first) % data_count
    spots = image_offsets[0] + order * tile_tok
    spots = spots[:, None] + jnp.arange(tile_tok, dtype=jnp.int32)[None, :]
    spots = jnp.where((order < my_count)[:, None], spots, -1).reshape(1, -1)
    gain = lax.dynamic_slice_in_dim(attn_gain, tensor_index * part_model, part_model, 0)
    sequence = sequences(
        spots, text_rows[0], received, gain[None, :], data_count, tensor_count, mid
    )
    product = product_blocks(sequence, weight, mid)
    context = attend(product, w_query.shape[1])
    return context[None]


def solution(mesh):
    in_specs = (
        P(None, "dp", None, "tensor"),
        P(),
        P(),
        P("dp", None, "tensor"),
        P("dp", None, "tensor"),
        P(),
        P("dp", "tensor"),
        P("dp", None, "tensor"),
        P(),
        P("dp"),
    )
    out_specs = P("dp", None, "tensor")
    return jax.shard_map(
        per_device, mesh=mesh, in_specs=in_specs, out_specs=out_specs, check_vma=False
    )
```

time: 522 us -> 498 us (0.954)
  local copies, waits for them, and re-layouts: 57.1 us -> 23.1 us
  Pallas kernels: 423 us -> 454 us
  other arithmetic: 12.9 us -> 5.2 us
  matrix products: 6.66 us -> 0 us
    pallas_call x5, Pallas kernels: 414 us -> 445 us  [the longest x1 132 us: product_blocks(): pl.pallas_call(functools.partial(product_kernel, mid, math.gcd(columns, 5...]
    dynamic_update_slice x3 -> x0, local copies, waits for them, and re-layouts: 20 us -> none  [the longest x2 13.1 us: per_device(): whole = lax.dynamic_update_slice_in_dim(whole, piece, start, 2)]
    reshape x6 -> x5, local copies, waits for them, and re-layouts: 19.3 us -> 2.79 us  [the longest x3 2.6 us: arranged(): parts.transpose(order).reshape((far_here,) + rows.shape[:lead] + (-1,))]
    dot_general x1 -> x0, matrix products: 6.66 us -> none  [per_device(): jnp.dot(blocks.reshape(data_count * token_count, merge_count * feature),...]
    another operation x1 -> x3, local copies, waits for them, and re-layouts: 0.08 us -> 5.33 us  [the longest x2 5.25 us: arranged(): parts = rows.reshape(rows.shape[:-1] + split)]
    unnamed x23 -> x19, local copies, waits for them, and re-layouts: 14 us -> 9.86 us
  transfers between devices with their start and end apart: 3 -> 1, of which waited for: 1 -> 0; matrix products, arithmetic and copies ran while one was open for 12% -> 3% of each run, Pallas kernels for 55% -> 63%
where the time goes in v1:
time: 498 us; the launch traced here: 496 us
  Pallas kernels  454 us (91%)
  local copies, waits for them, and re-layouts  23.1 us (5%)
  between operations  14.4 us (3%)
  other arithmetic  5.2 us (1%)
    pallas_call x1, Pallas kernels, product_blocks(): pl.pallas_call(functools.partial(product_kernel, mid, math.gcd(columns, 5...  132 us
    pallas_call x1, Pallas kernels, project(): pl.pallas_call(functools.partial(project_kernel, mid, math.gcd(columns, 5...  113 us
    pallas_call x1, Pallas kernels, front(): pl.pallas_call(functools.partial(front_kernel, mid), out_shape=(jax.Shape...  112 us
    pallas_call x1, Pallas kernels, sequences(): pl.pallas_call(functools.partial(sequence_kernel, mid, math.gcd(seq_len,...  47.9 us
    pallas_call x1, Pallas kernels, route(): pl.pallas_call(functools.partial(route_kernel, mid), out_shape=jax.ShapeD...  40.6 us
  transfers between devices with their start and end apart: 1, of which 0 were waited for; matrix products, arithmetic and copies ran while one was open for 3% of the time, Pallas kernels for 63%

profile of v1, /device:TPU:10, one launch (start us, length us, event | category | flops | bytes accessed | tf_op | source)
XLA Modules:
  0.0 496.4 jit_solution(13293580473051148573)
XLA Ops:
  6.5 1.6 copy.19
  8.2 0.3 copy-done.4
  8.4 1.9 pad_maximum_fusion
  10.6 0.1 reduce
  10.7 0.7 fusion.9
  11.4 0.1 compare_select_fusion
  11.6 0.1 constant_dynamic-slice_fusion
  11.7 0.1 reshape.460
  11.8 0.1 reshape.461.gain_ref
  11.9 0.1 reshape.462
  12.0 0.1 reshape.463.bias_ref
  12.2 4.1 copy.18
  16.3 2.7 reshape_reshape.3
  19.0 2.5 copy.21
  21.5 2.4 reshape.459.x_ref
  24.0 1.1 copy-done.3
  25.1 111.9 %shard_map.100 = (bf16[4,400,1024]{2,1,0:T(8,128)(2,1)S(1)}, bf16[4,4,64,1600]{3,2,1,0:T(8,128)(2,1)S(1)}) custom-call(bf16[2,64,1600]{2,1,0:T(8,128)(2,1)S(1)} %copy-done.3, f32[2,1600]{1,0:T(2,128)S(1)} %reshape.461.gain_ref, f32[2,1600]{1,0:T(2,128)S(1)} %reshape.463.bias_ref, bf16[400,4096]{1,0:T(8,128)(2,1)S(1)} %bitcast.21), custom_call_target="tpu_custom_call" | custom-call | bytes 83886080 | tf_op jit(solution)/shard_map/pallas_call | solution.py:225
  137.0 112.8 %shard_map.101 = bf16[256,1024]{1,0:T(8,128)(2,1)S(1)} custom-call(bf16[4,4,64,1600]{3,2,1,0:T(8,128)(2,1)S(1)} %get-tuple-element.7.vg_ref, bf16[1600,1024]{1,0:T(8,128)(2,1)S(1)} %bitcast.27), custom_call_target="tpu_custom_call" | custom-call | flops 3355443200 | bytes 83886080 | tf_op jit(solution)/shard_map/pallas_call | solution.py:314
  249.9 0.6 gather_fusion
  250.5 40.6 %shard_map.102 = bf16[4,4,32,1024]{3,2,1,0:T(8,128)(2,1)S(1)} custom-call(bf16[16,32,1024]{2,1,0:T(8,128)(2,1)S(1)} %bitcast.22), custom_call_target="tpu_custom_call" | custom-call | bytes 41943040 | tf_op jit(solution)/shard_map/pallas_call | solution.py:372
  291.1 0.7 add_subtract_fusion
  291.8 0.1 reshape.471
  292.5 0.6 broadcast_compare_fusion
  293.2 0.1 select_n.158.spot_ref
  293.4 1.9 copy-done.2
  295.3 47.9 %shard_map.103.a_ref = bf16[2,4,384,1024]{3,2,1,0:T(8,128)(2,1)S(1)} custom-call(s32[1,128]{1,0:T(1,128)S(1)} %select_n.158.spot_ref, bf16[384,4096]{1,0:T(8,128)(2,1)S(1)} %bitcast.24, bf16[4,128,1024]{2,1,0:T(8,128)(2,1)S(1)} %bitcast.23, f32[1,4096]{1,0:T(1,128)S(1)} %bitcast.26), custom_call_target="tpu_custom_call" | custom-call | bytes 104857600 | tf_op jit(solution)/shard_map/pallas_call | solution.py:499
  343.1 2.6 copy-done.1
  345.7 0.7 fusion.2
  346.5 0.2 pad_maximum_fusion.1
  346.7 131.6 %shard_map.104.q_ref.k_ref.v_ref = f32[384,3072]{1,0:T(8,128)} custom-call(bf16[2,4,384,1024]{3,2,1,0:T(8,128)(2,1)} %copy-done.1, bf16[2048,3072]{1,0:T(8,128)(2,1)} %all-gather.2.cloned.1.call-done.w_ref), custom_call_target="tpu_custom_call" | custom-call | flops 19327352832 | bytes 209715200 | tf_op jit(solution)/shard_map/pallas_call | solution.py:582
  478.3 2.3 copy-done
  480.6 8.9 %shard_map.105 = bf16[384,2048]{1,0:T(8,128)(2,1)} custom-call(f32[384,3072]{1,0:T(8,128)S(1)} %copy-done, f32[384,3072]{1,0:T(8,128)S(1)} %copy-done, f32[384,3072]{1,0:T(8,128)S(1)} %copy-done, f32[384,128]{1,0:T(8,128)S(1)} %get-tuple-element.23.cos_ref, f32[384,128]{1,0:T(8,128)S(1)} %get-tuple-element.24.sin_ref), custom_call_target="tpu_custom_call" | custom-call | tf_op jit(solution)/shard_map/pallas_call | solution.py:643
  (30 shorter events, 0.4 us)
Async XLA Ops:
  6.5 1.9 copy-start.4
  6.5 340.2 %all-gather.2.cloned.1.call-start = ((), (), s32[]{:S(2)}) async-start(), calls=%async_computation | async-start | bytes 15728640 | tf_op jit(solution)/shard_map/all_gather | solution.py:685
  8.4 2.0 copy-start.8
  8.4 3.1 copy-start.6
  8.4 3.2 copy-start.7
  24.0 1.1 copy-start.3
  249.9 43.5 %copy-start.5 = (f32[8192]{0:T(1024)S(1)}, f32[8192]{0:T(1024)}, u32[]{:S(2)}) copy-start(f32[8192]{0:T(1024)} %param.15) | copy-start | bytes 98308
  293.4 1.9 copy-start.2
  343.1 2.6 copy-start.1
  478.3 2.3 copy-start
Sparse Core Ops, SparseCore 0:
  10.5 297.9 all-gather.1

commit v2 on v1

--- a/solution.py
+++ b/solution.py
@@ -71,9 +71,146 @@
     )
 
 
-def front_kernel(mid, x_ref, gain_ref, bias_ref, pw_ref, pwg_ref, vg_ref, normed, stat_out,
-                 stat_in, pw_send, pw_recv, st_send, st_recv, far_send, far_recv, near_send,
-                 near_recv, twin_send, twin_recv):
+def flip(index, bits):
+    bit = 1
+    while bit <= bits:
+        if bits & bit:
+            index = index + bit - 2 * bit * (index // bit % 2)
+        bit *= 2
+    return index
+
+
+def gather_items(far_count):
+    items, masks, bit = [], [0], far_count // 2
+    while bit:
+        items += [(bit, mask) for mask in masks]
+        masks = masks + [mask | bit for mask in masks]
+        bit //= 2
+    return items
+
+
+def gather_plan(far_count, chunks):
+    third = chunks // 3
+    high = far_count // 2
+    items = gather_items(far_count)
+    plan = {"front": [], "sequence": [], "product": []}
+    have = {chunk: {0} for chunk in range(chunks)}
+    for name, first, others in (
+        ("front", range(third), range(2 * third)),
+        ("sequence", range(third, 2 * third), range(2 * third, chunks)),
+    ):
+        held = {chunk: set(masks) for chunk, masks in have.items()}
+        done = [job for jobs in plan.values() for job in jobs]
+        for chunk in range(chunks):
+            for bit, mask in items:
+                wanted = (chunk in first) if bit == high else (chunk in others)
+                if mask:
+                    wanted = name == "sequence" and chunk < third and mask in held[chunk]
+                if wanted and (bit, mask, chunk) not in done:
+                    plan[name].append((bit, mask, chunk))
+                    have[chunk].add(bit | mask)
+    done = plan["front"] + plan["sequence"]
+    for chunk in range(chunks):
+        plan["product"] += [
+            (bit, mask, chunk) for bit, mask in items if (bit, mask, chunk) not in done
+        ]
+    return plan, have
+
+
+def chunk_at(chunk, tile, refs, lead):
+    start = chunk * tile
+    for ref in refs:
+        width = ref.shape[-1]
+        if start < width:
+            part = pl.ds(start, tile)
+            return ref.at[:, part] if lead is None else ref.at[lead, :, part]
+        start -= width
+
+
+def weight_copies(mid, tile, jobs, own_refs, got_refs, send, recv):
+    me, my_far, _ = here(mid)
+    copies = []
+    for at, (bit, mask, chunk) in enumerate(jobs):
+        block = flip(my_far, mask)
+        source = chunk_at(chunk, tile, got_refs, block) if mask else chunk_at(
+            chunk, tile, own_refs, None
+        )
+        copies.append(
+            remote(
+                source,
+                chunk_at(chunk, tile, got_refs, block),
+                send.at[at],
+                recv.at[at],
+                {"dp": join(me, flip(my_far, bit), mid)},
+            )
+        )
+    return copies
+
+
+class Halving:
+    def __init__(self, bits, index, device, rows, out_ref, in_ref, acc_ref, own_ref, send, recv):
+        self.bits, self.index, self.device, self.rows = bits, index, device, rows
+        self.out_ref, self.in_ref, self.acc_ref, self.own_ref = out_ref, in_ref, acc_ref, own_ref
+        self.send, self.recv = send, recv
+        size = 1 << len(bits)
+        self.stage_of = {
+            mask: min(at for at, bit in enumerate(bits) if mask & bit) for mask in range(1, size)
+        }
+        later = [mask for mask in range(1, size) if self.stage_of[mask]]
+        self.slot = {mask: at for at, mask in enumerate(later)}
+        self.copies = []
+
+    def masks(self, stage):
+        return [mask for mask, at in self.stage_of.items() if at == stage]
+
+    def start(self, stage):
+        bit = self.bits[stage]
+        for mask in self.masks(stage):
+            copy = remote(
+                self.out_ref.at[mask - 1],
+                self.in_ref.at[mask - 1],
+                self.send.at[mask - 1],
+                self.recv.at[mask - 1],
+                self.device(flip(self.index, bit)),
+            )
+            copy.start()
+            self.copies.append((stage, copy))
+
+    def receive(self, stage):
+        for at, copy in self.copies:
+            if at == stage:
+                copy.wait_recv()
+        rows, bit = self.rows, self.bits[stage]
+        last = stage + 1 == len(self.bits)
+
+        def add(at, carry):
+            window = pl.ds(pl.multiple_of(at * rows, rows), rows)
+            for mask in self.masks(stage):
+                value = self.in_ref[mask - 1, window, :].astype(jnp.float32)
+                rest = mask - bit
+                if not rest:
+                    self.own_ref[window, :] = self.own_ref[window, :] + value
+                else:
+                    value = self.acc_ref[self.slot[rest], window, :] + value
+                    if self.stage_of[rest] == stage + 1:
+                        self.out_ref[rest - 1, window, :] = value.astype(self.out_ref.dtype)
+                    else:
+                        self.acc_ref[self.slot[rest], window, :] = value
+            return carry
+
+        lax.fori_loop(0, self.own_ref.shape[0] // rows, add, 0)
+        if not last:
+            self.start(stage + 1)
+
+    def finish(self):
+        for _, copy in self.copies:
+            copy.wait_send()
+
+
+def front_kernel(mid, tile, jobs, x_ref, gain_ref, bias_ref, pw_ref, wq_ref, wkv_ref, pwg_ref,
+                 vg_ref, gq_ref, gkv_ref, normed, stat_out, stat_in, pw_send, pw_recv, st_send,
+                 st_recv, far_send, far_recv, near_send, near_recv, twin_send, twin_recv, w_send,
+                 w_recv):
     blocks, tokens, width = x_ref.shape
     far_count = vg_ref.shape[1]
     rows, wide = pwg_ref.shape[1:]
@@ -92,6 +229,12 @@
         )
         copy.start()
         pw_copies.append(copy)
+    w_copies = weight_copies(
+        mid, tile, jobs, (wq_ref, wkv_ref), (gq_ref, gkv_ref), w_send, w_recv
+    )
+    early = len(w_copies) // 3
+    for copy in w_copies[:early]:
+        copy.start()
 
     count = blocks * width
     total = jnp.zeros((tokens, 1), jnp.float32)
@@ -146,6 +289,8 @@
         def _():
             vg_ref[me, my_far] = normed[at]
 
+    for copy in w_copies[early:]:
+        copy.start()
     holder = my_far // blocks == tensor_index
 
     def twin_copy(ahead, step, block):
@@ -212,24 +357,27 @@
         pl.when(jnp.logical_not(mine))(copy.wait_send)
     for copy in stat_copies:
         copy.wait_send()
-    for copy in pw_copies:
+    for copy in pw_copies + w_copies:
         copy.wait()
 
 
-def front(x, gain, bias, proj, data_count, tensor_count, mid):
+def front(x, gain, bias, proj, w_query, w_kv, tile, jobs, data_count, tensor_count, mid):
     blocks, tokens, width = x.shape
     far_count = data_count // NEAR
     rows, columns = proj.shape
     vmem = pl.BlockSpec(memory_space=pltpu.VMEM)
+    anywhere = pl.BlockSpec(memory_space=pl.ANY)
     dma = pltpu.SemaphoreType.DMA
     return pl.pallas_call(
-        functools.partial(front_kernel, mid),
+        functools.partial(front_kernel, mid, tile, jobs),
         out_shape=(
             jax.ShapeDtypeStruct((NEAR, rows, columns // NEAR), proj.dtype),
             jax.ShapeDtypeStruct((NEAR, far_count, tokens, width), x.dtype),
+            jax.ShapeDtypeStruct((far_count,) + w_query.shape, w_query.dtype),
+            jax.ShapeDtypeStruct((far_count,) + w_kv.shape, w_kv.dtype),
         ),
-        in_specs=[vmem] * 4,
-        out_specs=(vmem, vmem),
+        in_specs=[vmem] * 4 + [anywhere] * 2,
+        out_specs=(vmem, vmem, anywhere, anywhere),
         scratch_shapes=[
             pltpu.VMEM((blocks, tokens, width), x.dtype),
             pltpu.VMEM((2, tokens, 128), jnp.float32),
@@ -244,84 +392,73 @@
             dma((NEAR - 1,)),
             dma((tensor_count - 1, NEAR)),
             dma((NEAR,)),
+            dma((len(jobs),)),
+            dma((len(jobs),)),
         ],
         compiler_params=pltpu.CompilerParams(
             collective_id=0, has_side_effects=True, vmem_limit_bytes=40 << 20
         ),
         cost_estimate=pl.CostEstimate(flops=0, bytes_accessed=80 << 20, transcendentals=0),
-    )(x, gain, bias, proj)
-
-
-def far_order(far_count):
-    half = far_count // 2
-    return [half] + [s for s in range(1, far_count) if s != half]
-
-
-def project_kernel(mid, tile, rows, vg_ref, pw_ref, o_ref, total, leaving, held, send, recv):
+    )(x, gain, bias, proj, w_query, w_kv)
+
+
+def project_kernel(mid, tile, vg_ref, pw_ref, o_ref, own, acc, out, held, send, recv):
     near, far_count, tokens, width = vg_ref.shape
     me, my_far, _ = here(mid)
-    columns = o_ref.shape[1]
-
-    def compute(block, dst_ref):
-        def one(at, carry):
-            part = pl.ds(pl.multiple_of(at * tile, tile), tile)
-            term = jnp.dot(
-                vg_ref[:, block].reshape(near * tokens, width),
-                pw_ref[:, part],
-                preferred_element_type=jnp.float32,
-            )
-            dst_ref[:, part] = term.astype(dst_ref.dtype)
-            return carry
-
-        lax.fori_loop(0, columns // tile, one, 0)
+    chunks = own.shape[0]
+    bits = []
+    while 1 << len(bits) < far_count:
+        bits.append(1 << len(bits))
+
+    def compute(mask, chunk, dst_ref):
+        term = jnp.dot(
+            vg_ref[:, flip(my_far, mask)].reshape(near * tokens, width),
+            pw_ref[:, pl.ds(chunk * tile, tile)],
+            preferred_element_type=jnp.float32,
+        )
+        dst_ref[...] = term.astype(dst_ref.dtype)
 
     meet(mid, near=False, twin=False)
-    copies = []
-    for step in far_order(far_count):
-        target = (my_far + step) % far_count
-        compute(target, leaving.at[step - 1])
-        copy = remote(
-            leaving.at[step - 1],
-            held.at[step - 1],
-            send.at[step - 1],
-            recv.at[step - 1],
-            {"dp": join(me, target, mid)},
-        )
-        copy.start()
-        copies.append(copy)
-    compute(my_far, total)
-    for copy in copies:
-        copy.wait_recv()
-
-    def add(at, carry):
-        window = pl.ds(pl.multiple_of(at * rows, rows), rows)
-        value = total[window, :]
-        for step in range(1, far_count):
-            value = value + held[step - 1, window, :].astype(jnp.float32)
-        o_ref[window, :] = value.astype(o_ref.dtype)
-        return carry
-
-    lax.fori_loop(0, o_ref.shape[0] // rows, add, 0)
-    for copy in copies:
-        copy.wait_send()
+    sums = []
+    for chunk in range(chunks):
+        one = Halving(
+            bits, my_far, lambda far: {"dp": join(me, far, mid)}, 32, out.at[chunk],
+            held.at[chunk], acc.at[chunk], own.at[chunk], send.at[chunk], recv.at[chunk],
+        )
+        for mask in one.masks(0):
+            compute(mask, chunk, out.at[chunk, mask - 1])
+        one.start(0)
+        sums.append(one)
+    for chunk, one in enumerate(sums):
+        for mask, slot in one.slot.items():
+            compute(mask, chunk, acc.at[chunk, slot])
+        compute(0, chunk, own.at[chunk])
+    for stage in range(len(bits)):
+        for one in sums:
+            one.receive(stage)
+    for chunk, one in enumerate(sums):
+        o_ref[:, pl.ds(chunk * tile, tile)] = own[chunk].astype(o_ref.dtype)
+        one.finish()
 
 
 def project(vg, pw, mid):
     near, far_count, tokens, width = vg.shape
     columns = pw.shape[1]
-    shape = (near * tokens, columns)
+    tile = math.gcd(columns, 512)
+    chunks, rows = columns // tile, near * tokens
     dma = pltpu.SemaphoreType.DMA
     return pl.pallas_call(
-        functools.partial(project_kernel, mid, math.gcd(columns, 512), 16),
-        out_shape=jax.ShapeDtypeStruct(shape, vg.dtype),
+        functools.partial(project_kernel, mid, tile),
+        out_shape=jax.ShapeDtypeStruct((rows, columns), vg.dtype),
         in_specs=[pl.BlockSpec(memory_space=pltpu.VMEM)] * 2,
         out_specs=pl.BlockSpec(memory_space=pltpu.VMEM),
         scratch_shapes=[
-            pltpu.VMEM(shape, jnp.float32),
-            pltpu.VMEM((far_count - 1,) + shape, vg.dtype),
-            pltpu.VMEM((far_count - 1,) + shape, vg.dtype),
-            dma((far_count - 1,)),
-            dma((far_count - 1,)),
+            pltpu.VMEM((chunks, rows, tile), jnp.float32),
+            pltpu.VMEM((chunks, far_count // 2 - 1, rows, tile), jnp.float32),
+            pltpu.VMEM((chunks, far_count - 1, rows, tile), vg.dtype),
+            pltpu.VMEM((chunks, far_count - 1, rows, tile), vg.dtype),
+            dma((chunks, far_count - 1)),
+            dma((chunks, far_count - 1)),
         ],
         compiler_params=pltpu.CompilerParams(
             collective_id=1, has_side_effects=True, vmem_limit_bytes=40 << 20
@@ -382,14 +519,22 @@
     )(tiles)
 
 
-def sequence_kernel(mid, rows, spot_ref, text_ref, got_ref, gain_ref, a_ref, seq, sums, sums_in,
-                    leaving, st_send, st_recv, near_send, near_recv, twin_send, twin_recv):
-    tensor_count, _, seq_len, held = a_ref.shape
+def sequence_kernel(mid, rows, tile, jobs, spot_ref, text_ref, got_ref, gain_ref, wq_ref,
+                    wkv_ref, gq_in, gkv_in, a_ref, gq_ref, gkv_ref, seq, sums, sums_in, leaving,
+                    st_send, st_recv, near_send, near_recv, twin_send, twin_recv, w_send, w_recv):
+    _, seq_len, depth = a_ref.shape
     near, _, wide = got_ref.shape
+    tensor_count = lax.axis_size("tensor")
+    held = depth // tensor_count
     model_width = text_ref.shape[1] * tensor_count
     me, my_far, tensor_index = here(mid)
     shift = held // (lax.axis_size("dp") // NEAR // tensor_count)
-    meet(mid, far=False)
+    meet(mid)
+    w_copies = weight_copies(
+        mid, tile, jobs, (wq_ref, wkv_ref), (gq_ref, gkv_ref), w_send, w_recv
+    )
+    for copy in w_copies:
+        copy.start()
 
     def fill(at, carry):
         window = pl.ds(pl.multiple_of(at * rows, rows), rows)
@@ -432,22 +577,25 @@
             for part in range(held // shift):
                 lanes = pl.ds(pl.multiple_of(join(target, part, mid) * shift, shift), shift)
                 value = seq[window, lanes].astype(jnp.float32) * scale * gain_ref[:, lanes]
-                store(window, pl.ds(part * shift, shift), value.astype(jnp.bfloat16))
+                store(window, part * shift, value.astype(jnp.bfloat16))
             return carry
 
         lax.fori_loop(0, seq_len // rows, one, 0)
+
+    def lanes_of(owner):
+        return pl.ds(pl.multiple_of(owner * held, held), held)
 
     near_copies, twin_copies = [], []
     for step in range(1, NEAR):
-        target = (me + step) % NEAR
-
-        def leave(window, lanes, value):
-            leaving[step - 1, window, lanes] = value
+        target = flip(me, step)
+
+        def leave(window, start, value):
+            leaving[step - 1, window, pl.ds(start, shift)] = value
 
         norm(target, leave)
         copy = remote(
             leaving.at[step - 1],
-            a_ref.at[tensor_index, me],
+            a_ref.at[me, :, lanes_of(tensor_index)],
             near_send.at[step - 1],
             near_recv.at[step - 1],
             {"dp": join(target, my_far, mid)},
@@ -455,16 +603,17 @@
         copy.start()
         near_copies.append(copy)
 
-    def stay(window, lanes, value):
-        a_ref[tensor_index, me, window, lanes] = value
+    def stay(window, start, value):
+        lanes = pl.ds(pl.multiple_of(tensor_index * held + start, shift), shift)
+        a_ref[me, window, lanes] = value
 
     norm(me, stay)
 
     def twin_copy(ahead, step, owner):
-        block = (me + NEAR - step) % NEAR
+        block = flip(me, step)
         return remote(
-            a_ref.at[owner, block],
-            a_ref.at[owner, block],
+            a_ref.at[block, :, lanes_of(owner)],
+            a_ref.at[block, :, lanes_of(owner)],
             twin_send.at[ahead - 1, step],
             twin_recv.at[ahead - 1, step],
             {"tensor": (tensor_index + ahead) % tensor_count},
@@ -472,13 +621,7 @@
 
     for step in range(NEAR):
         if step:
-            remote(
-                leaving.at[step - 1],
-                a_ref.at[tensor_index, (me + NEAR - step) % NEAR],
-                near_send.at[step - 1],
-                near_recv.at[step - 1],
-                {"dp": join((me + step) % NEAR, my_far, mid)},
-            ).wait_recv()
+            near_copies[step - 1].wait_recv()
         for ahead in range(1, tensor_count):
             copy = twin_copy(ahead, step, tensor_index)
             copy.start()
@@ -489,18 +632,23 @@
             twin_copy(ahead, step, owner).wait_recv()
     for copy in near_copies + twin_copies + stat_copies:
         copy.wait_send()
-
-
-def sequences(spots, text, got, gain, data_count, tensor_count, mid):
+    for copy in w_copies:
+        copy.wait()
+
+
+def sequences(spots, text, got, gain, weights, gathered, tile, jobs, tensor_count, mid):
     seq_len, part_model = text.shape
     held = part_model // NEAR
     vmem = pl.BlockSpec(memory_space=pltpu.VMEM)
+    anywhere = pl.BlockSpec(memory_space=pl.ANY)
     dma = pltpu.SemaphoreType.DMA
     return pl.pallas_call(
-        functools.partial(sequence_kernel, mid, math.gcd(seq_len, 32)),
-        out_shape=jax.ShapeDtypeStruct((tensor_count, NEAR, seq_len, held), text.dtype),
-        in_specs=[vmem] * 4,
-        out_specs=vmem,
+        functools.partial(sequence_kernel, mid, math.gcd(seq_len, 32), tile, jobs),
+        out_shape=(jax.ShapeDtypeStruct((NEAR, seq_len, held * tensor_count), text.dtype),)
+        + tuple(jax.ShapeDtypeStruct(one.shape, one.dtype) for one in gathered),
+        in_specs=[vmem] * 4 + [anywhere] * 4,
+        out_specs=(vmem, anywhere, anywhere),
+        input_output_aliases={6: 1, 7: 2},
         scratch_shapes=[
             pltpu.VMEM((seq_len, part_model), text.dtype),
             pltpu.VMEM((seq_len, 128), jnp.float32),
@@ -512,93 +660,159 @@
             dma((NEAR - 1,)),
             dma((tensor_count - 1, NEAR)),
             dma((tensor_count - 1, NEAR)),
+            dma((len(jobs),)),
+            dma((len(jobs),)),
         ],
         compiler_params=pltpu.CompilerParams(
             collective_id=3, has_side_effects=True, vmem_limit_bytes=40 << 20
         ),
         cost_estimate=pl.CostEstimate(flops=0, bytes_accessed=100 << 20, transcendentals=0),
-    )(spots, text, got, gain)
-
-
-def product_kernel(mid, tile, rows, a_ref, w_ref, o_ref, leaving, held, send_sem, recv_sem):
-    count, _, seq_len, depth = a_ref.shape
+    )(spots, text, got, gain, *weights, *gathered)
+
+
+def product_kernel(mid, tile, jobs, have, a_ref, wq_ref, wkv_ref, gq_ref, gkv_ref, o_ref, w, acc,
+                   out, held, send, recv, w_send, w_recv, load_sem):
+    _, seq_len, _ = a_ref.shape
+    depth = wq_ref.shape[0]
+    far_count = gq_ref.shape[0]
     me, my_far, _ = here(mid)
-    tiles = o_ref.shape[1] // tile
-
-    def compute(block, dst_ref, low, high):
-        def one(at, carry):
-            part = pl.ds(pl.multiple_of(at * tile, tile), tile)
-            total = None
-            for piece in range(count):
-                term = jnp.dot(
-                    a_ref[piece, block],
-                    w_ref[pl.ds(piece * depth, depth), part],
-                    preferred_element_type=jnp.float32,
-                )
-                total = term if total is None else total + term
-            dst_ref[:, part] = total.astype(dst_ref.dtype)
-            return carry
-
-        lax.fori_loop(low, high, one, 0)
-
-    meet(mid, far=False, twin=False)
-    copies = []
-    for step in range(1, NEAR + 1):
-        block = (me + step) % NEAR
-        dst_ref = leaving.at[step - 1] if step < NEAR else o_ref
-        compute(block, dst_ref, 0, 1)
-        if copies:
-            copies[-1].start()
-        compute(block, dst_ref, 1, tiles)
-        if step < NEAR:
-            copies.append(
-                remote(
-                    leaving.at[step - 1],
-                    held.at[step - 1],
-                    send_sem.at[step - 1],
-                    recv_sem.at[step - 1],
-                    {"dp": join(block, my_far, mid)},
-                )
+    chunks = len(have)
+    own_refs, got_refs = (wq_ref, wkv_ref), (gq_ref, gkv_ref)
+
+    def place(mask, chunk):
+        rows = pl.ds(pl.multiple_of(flip(my_far, mask) * depth, depth), depth)
+        return w.at[rows, pl.ds(chunk * tile, tile)]
+
+    def local(mask, chunk):
+        if mask:
+            return chunk_at(chunk, tile, got_refs, flip(my_far, mask))
+        return chunk_at(chunk, tile, own_refs, None)
+
+    loads = {}
+    for chunk in range(chunks):
+        for mask in sorted(have[chunk]):
+            loads[mask, chunk] = pltpu.make_async_copy(
+                local(mask, chunk), place(mask, chunk), load_sem.at[chunk, mask]
             )
-    for copy in copies:
-        copy.wait_recv()
-
-    def add(at, carry):
-        window = pl.ds(pl.multiple_of(at * rows, rows), rows)
-        total = o_ref[window, :]
-        for step in range(1, NEAR):
-            total = total + held[step - 1, window, :].astype(jnp.float32)
-        o_ref[window, :] = total
-        return carry
-
-    lax.fori_loop(0, seq_len // rows, add, 0)
-    for copy in copies:
+            loads[mask, chunk].start()
+
+    meet(mid, twin=False)
+    arriving, waiting = {}, {chunk: [] for chunk in range(chunks)}
+    for at, (bit, mask, chunk) in enumerate(jobs):
+        kept = mask in have[chunk]
+        copy = remote(
+            local(mask, chunk) if kept else place(mask, chunk),
+            place(mask, chunk),
+            w_send.at[at],
+            w_recv.at[at],
+            {"dp": join(me, flip(my_far, bit), mid)},
+        )
+        arriving[bit | mask, chunk] = copy
+        if kept:
+            copy.start()
+        else:
+            waiting[chunk].append((mask, copy))
+    seen = set()
+
+    def ensure(mask, chunk):
+        if (mask, chunk) not in seen:
+            seen.add((mask, chunk))
+            if (mask, chunk) in loads:
+                loads[mask, chunk].wait()
+            else:
+                arriving[mask, chunk].wait_recv()
+
+    def forward(chunk):
+        for mask, copy in waiting.pop(chunk, ()):
+            ensure(mask, chunk)
+            copy.start()
+
+    sums = []
+
+    def compute(chunk):
+        forward(chunk)
+        for mask in range(far_count):
+            ensure(mask, chunk)
+        part = pl.ds(chunk * tile, tile)
+        bits = (1, 2) if chunk % 2 else (2, 1)
+        one = Halving(
+            bits, me, lambda near: {"dp": join(near, my_far, mid)}, math.gcd(seq_len, 32),
+            out.at[chunk], held.at[chunk], acc.at[chunk], o_ref.at[:, part], send.at[chunk],
+            recv.at[chunk],
+        )
+
+        def fill(mask, dst_ref):
+            term = jnp.dot(
+                a_ref[flip(me, mask)], w[:, part], preferred_element_type=jnp.float32
+            )
+            dst_ref[...] = term.astype(dst_ref.dtype)
+
+        for mask in one.masks(0):
+            fill(mask, out.at[chunk, mask - 1])
+        one.start(0)
+        for mask, slot in one.slot.items():
+            fill(mask, acc.at[chunk, slot])
+        fill(0, o_ref.at[:, part])
+        sums.append(one)
+
+    done = {0: 0, 1: 0}
+
+    def reduce(stage, upto):
+        for one in sums[done[stage] : upto]:
+            one.receive(stage)
+        done[stage] = max(done[stage], upto)
+
+    third = chunks // 3
+    for chunk in range(2 * third):
+        compute(chunk)
+    reduce(0, third)
+    for chunk in range(2 * third, chunks):
+        forward(chunk)
+        reduce(0, 2 * third)
+        if chunk > 2 * third:
+            reduce(1, 2 * third)
+        compute(chunk)
+    reduce(0, chunks)
+    reduce(1, chunks)
+    for one in sums:
+        one.finish()
+    for copy in arriving.values():
         copy.wait_send()
 
 
-def product_blocks(a, weight, mid):
-    count, _, seq_len, depth = a.shape
-    columns = weight.shape[1]
+def product_blocks(a, weights, gathered, tile, jobs, have, mid):
+    _, seq_len, depth = a.shape
+    columns = sum(one.shape[1] for one in weights)
+    chunks = columns // tile
+    vmem = pl.BlockSpec(memory_space=pltpu.VMEM)
+    anywhere = pl.BlockSpec(memory_space=pl.ANY)
+    far_count = gathered[0].shape[0]
+    dma = pltpu.SemaphoreType.DMA
     return pl.pallas_call(
-        functools.partial(product_kernel, mid, math.gcd(columns, 512), math.gcd(seq_len, 16)),
+        functools.partial(product_kernel, mid, tile, jobs, have),
         out_shape=jax.ShapeDtypeStruct((seq_len, columns), jnp.float32),
-        in_specs=[pl.BlockSpec(memory_space=pltpu.VMEM)] * 2,
-        out_specs=pl.BlockSpec(memory_space=pltpu.VMEM),
+        in_specs=[vmem] + [anywhere] * 4,
+        out_specs=vmem,
         scratch_shapes=[
-            pltpu.VMEM((NEAR - 1, seq_len, columns), jnp.bfloat16),
-            pltpu.VMEM((NEAR - 1, seq_len, columns), jnp.bfloat16),
-            pltpu.SemaphoreType.DMA((NEAR - 1,)),
-            pltpu.SemaphoreType.DMA((NEAR - 1,)),
+            pltpu.VMEM((depth, columns), jnp.bfloat16),
+            pltpu.VMEM((chunks, NEAR // 2 - 1, seq_len, tile), jnp.float32),
+            pltpu.VMEM((chunks, NEAR - 1, seq_len, tile), jnp.bfloat16),
+            pltpu.VMEM((chunks, NEAR - 1, seq_len, tile), jnp.bfloat16),
+            dma((chunks, NEAR - 1)),
+            dma((chunks, NEAR - 1)),
+            dma((len(jobs),)),
+            dma((len(jobs),)),
+            dma((chunks, far_count)),
         ],
         compiler_params=pltpu.CompilerParams(
             collective_id=4, has_side_effects=True, vmem_limit_bytes=56 << 20
         ),
         cost_estimate=pl.CostEstimate(
-            flops=2 * count * NEAR * seq_len * depth * columns,
+            flops=2 * NEAR * seq_len * depth * columns,
             bytes_accessed=200 << 20,
             transcendentals=0,
         ),
-    )(a, weight)
+    )(a, *weights, *gathered)
 
 
 def attend_kernel(group, q_ref, k_ref, v_ref, cos_ref, sin_ref, o_ref):
@@ -680,9 +894,10 @@
     far_count = data_count // NEAR
     far_here = far_count // tensor_count
     depth = w_query.shape[0]
-    groups = [[join(p, f, mid) for f in range(far_count)] for p in range(NEAR)]
-    weight = jnp.concatenate([w_query, key_value_weight.reshape(depth, -1)], axis=1)
-    weight = lax.all_gather(weight, "dp", axis=0, tiled=True, axis_index_groups=groups)
+    weights = (w_query, key_value_weight.reshape(depth, -1))
+    tile = math.gcd(512, *(one.shape[1] for one in weights))
+    chunks = sum(one.shape[1] for one in weights) // tile
+    plan, have = gather_plan(far_count, chunks)
 
     tops = far_here // mid
     split = (tops, 2, mid, 2, feature)
@@ -698,7 +913,9 @@
     bias = arranged(lax.dynamic_slice_in_dim(ln_bias, start, part_width, 1))
     rows_in = arranged(vis_rows.reshape(tokens, merge_count, part_width))
     proj = proj_weight.transpose(1, 0, 2).reshape(merge_count * feature, part_model)
-    proj, normed = front(rows_in, gain, bias, proj, data_count, tensor_count, mid)
+    proj, normed, *gathered = front(
+        rows_in, gain, bias, proj, *weights, tile, plan["front"], data_count, tensor_count, mid
+    )
     image = project(normed, proj.reshape(-1, proj.shape[2]), mid)
 
     max_tiles = 2 * tile_rows
@@ -723,10 +940,11 @@
     spots = spots[:, None] + jnp.arange(tile_tok, dtype=jnp.int32)[None, :]
     spots = jnp.where((order < my_count)[:, None], spots, -1).reshape(1, -1)
     gain = lax.dynamic_slice_in_dim(attn_gain, tensor_index * part_model, part_model, 0)
-    sequence = sequences(
-        spots, text_rows[0], received, gain[None, :], data_count, tensor_count, mid
+    sequence, *gathered = sequences(
+        spots, text_rows[0], received, gain[None, :], weights, gathered, tile,
+        plan["sequence"], tensor_count, mid,
     )
-    product = product_blocks(sequence, weight, mid)
+    product = product_blocks(sequence, weights, gathered, tile, plan["product"], have, mid)
     context = attend(product, w_query.shape[1])
     return context[None]
 

time: 498 us -> 393 us (0.79)
  Pallas kernels: 454 us -> 350 us
  between operations: 14.4 us -> 0.89 us
  local copies, waits for them, and re-layouts: 23.1 us -> 35.6 us
    pallas_call x3, Pallas kernels: 356 us -> 246 us  [the longest x1 120 us: product_blocks(): pl.pallas_call(functools.partial(product_kernel, mid, tile, jobs, have),...]
    pallas_call x1, Pallas kernels: 47.9 us -> 65.8 us  [sequences(): pl.pallas_call(functools.partial(sequence_kernel, mid, math.gcd(seq_len,...]
    pallas_call x1, Pallas kernels: 40.6 us -> 29.2 us  [route(): pl.pallas_call(functools.partial(route_kernel, mid), out_shape=jax.ShapeD...]
    unnamed x19 -> x29, local copies, waits for them, and re-layouts: 9.86 us -> 19 us
  transfers between devices with their start and end apart: 1 -> 0, of which waited for: 0 -> 0; matrix products, arithmetic and copies ran while one was open for 3% -> 0% of each run, Pallas kernels for 63% -> 0%
where the time goes in v2:
time: 393 us; the launch traced here: 390 us
  Pallas kernels  350 us (89%)
  local copies, waits for them, and re-layouts  35.6 us (9%)
    pallas_call x1, Pallas kernels, product_blocks(): pl.pallas_call(functools.partial(product_kernel, mid, tile, jobs, have),...  120 us
    pallas_call x1, Pallas kernels, front(): pl.pallas_call(functools.partial(front_kernel, mid, tile, jobs), out_shap...  88.7 us
    pallas_call x1, Pallas kernels, sequences(): pl.pallas_call(functools.partial(sequence_kernel, mid, math.gcd(seq_len,...  65.8 us
    pallas_call x1, Pallas kernels, project(): pl.pallas_call(functools.partial(project_kernel, mid, tile), out_shape=ja...  37.6 us
    pallas_call x1, Pallas kernels, route(): pl.pallas_call(functools.partial(route_kernel, mid), out_shape=jax.ShapeD...  29.2 us
    unnamed x29, local copies, waits for them, and re-layouts  19 us
    pallas_call x1, Pallas kernels, attend(): pl.pallas_call(functools.partial(attend_kernel, group), grid=(local_kv,),...  8.93 us

profile of v2, /device:TPU:10, one launch (start us, length us, event | category | flops | bytes accessed | tf_op | source)
XLA Modules:
  0.0 390.5 jit_solution(6619933097468489067)
XLA Ops:
  0.0 0.7 copy.16
  0.8 0.1 reduce
  0.9 1.3 fusion.9
  2.4 0.8 constant_dynamic-slice_fusion
  3.3 0.1 reshape.460
  3.7 2.4 copy.21
  6.1 4.1 %copy.20 = bf16[2,200,4096]{2,1,0:T(8,128)(2,1)S(1)} copy(bf16[2,200,4096]{2,0,1:T(2,128)(2,1)} %bitcast.31) | data formatting | bytes 6553600 | tf_op jit(solution)/shard_map/transpose | solution.py:915
  10.3 2.7 reshape_reshape.3
  13.0 2.4 copy.23
  15.4 2.3 reshape.459.x_ref
  17.7 1.2 copy-done.1
  19.0 1.6 copy-done.3
  20.5 1.0 copy-done.12
  21.6 88.7 %shard_map.100 = (bf16[4,400,1024]{2,1,0:T(8,128)(2,1)S(1)}, bf16[4,4,64,1600]{3,2,1,0:T(8,128)(2,1)S(1)}, bf16[4,512,2048]{2,1,0:T(8,128)(2,1)}, bf16[4,512,1024]{2,1,0:T(8,128)(2,1)}) custom-call(bf16[2,64,1600]{2,1,0:T(8,128)(2,1)S(1)} %copy-done.12, f32[2,1600]{1,0:T(2,128)S(1)} %reshape.461.gain_ref, f32[2,1600]{1,0:T(2,128)S(1)} %reshape.463.bias_ref, ...), custom_call_target="tpu_custom_call" | custom-call | bytes 83886080 | tf_op jit(solution)/shard_map/pallas_call | solution.py:371
  110.3 37.6 %shard_map.101 = bf16[256,1024]{1,0:T(8,128)(2,1)S(1)} custom-call(bf16[4,4,64,1600]{3,2,1,0:T(8,128)(2,1)S(1)} %get-tuple-element.12.vg_ref, bf16[1600,1024]{1,0:T(8,128)(2,1)S(1)} %bitcast.30), custom_call_target="tpu_custom_call" | custom-call | flops 3355443200 | bytes 83886080 | tf_op jit(solution)/shard_map/pallas_call | solution.py:450
  147.9 0.8 copy-done.11
  148.7 2.9 gather_fusion
  151.5 1.2 copy-done.9
  152.8 29.2 %shard_map.102 = bf16[4,4,32,1024]{3,2,1,0:T(8,128)(2,1)S(1)} custom-call(bf16[16,32,1024]{2,1,0:T(8,128)(2,1)S(1)} %bitcast.26), custom_call_target="tpu_custom_call" | custom-call | bytes 41943040 | tf_op jit(solution)/shard_map/pallas_call | solution.py:509
  182.0 1.0 copy-done.7
  183.0 0.6 add_subtract_fusion
  183.7 0.6 broadcast_compare_fusion
  185.3 2.2 copy-done.5
  187.4 1.2 copy-done.8
  188.7 1.9 copy-done.10
  190.6 65.8 %shard_map.103 = (bf16[4,384,2048]{2,1,0:T(8,128)(2,1)}, bf16[4,512,2048]{2,1,0:T(8,128)(2,1)}, bf16[4,512,1024]{2,1,0:T(8,128)(2,1)S(1)}) custom-call(s32[1,128]{1,0:T(1,128)S(1)} %select_n.158.spot_ref, bf16[384,4096]{1,0:T(8,128)(2,1)S(1)} %bitcast.27, bf16[4,128,1024]{2,1,0:T(8,128)(2,1)S(1)} %bitcast.25, ...), custom_call_target="tpu_custom_call", output_to_operand_aliasing={{1}: (6, {}), {2}: (7, {})} | custom-call | bytes 104857600 | tf_op jit(solution)/shard_map/pallas_call | solution.py:645
  256.4 2.0 copy-done.6
  258.4 119.8 %shard_map.104.q_ref.k_ref.v_ref = f32[384,3072]{1,0:T(8,128)} custom-call(bf16[4,384,2048]{2,1,0:T(8,128)(2,1)} %get-tuple-element.16.a_ref, bf16[512,2048]{1,0:T(8,128)(2,1)} %wq_ref.5, bf16[512,1024]{1,0:T(8,128)(2,1)} %bitcast.22, bf16[4,512,2048]{2,1,0:T(8,128)(2,1)} %get-tuple-element.17.gq_ref, bf16[4,512,1024]{2,1,0:T(8,128)(2,1)} %copy-done.6), custom_call_target="tpu_custom_call" | custom-call | flops 19327352832 | bytes 209715200 | tf_op jit(solution)/shard_map/pallas_call | solution.py:791
  378.3 0.7 fusion.2
  379.0 0.2 pad_maximum_fusion
  379.2 2.3 copy-done
  381.5 8.9 %shard_map.105 = bf16[384,2048]{1,0:T(8,128)(2,1)} custom-call(f32[384,3072]{1,0:T(8,128)S(1)} %copy-done, f32[384,3072]{1,0:T(8,128)S(1)} %copy-done, f32[384,3072]{1,0:T(8,128)S(1)} %copy-done, f32[384,128]{1,0:T(8,128)S(1)} %get-tuple-element.33.cos_ref, f32[384,128]{1,0:T(8,128)S(1)} %get-tuple-element.34.sin_ref), custom_call_target="tpu_custom_call" | custom-call | tf_op jit(solution)/shard_map/pallas_call | solution.py:857
  (36 shorter events, 0.8 us)
Async XLA Ops:
  17.7 1.2 copy-start.1
  19.0 1.6 copy-start.3
  20.5 1.0 copy-start.12
  110.3 75.0 %copy-start.13 = (f32[8192]{0:T(1024)S(1)}, f32[8192]{0:T(1024)}, u32[]{:S(2)}) copy-start(f32[8192]{0:T(1024)} %param.15) | copy-start | bytes 98308
  147.9 0.8 copy-start.11
  148.7 36.6 %copy-start.2 = (bf16[64,8,2,512]{3,1,2,0:T(8,128)(2,1)S(1)}, bf16[64,8,2,512]{3,1,2,0:T(8,128)(2,1)}, u32[]{:S(2)}) copy-start(bf16[64,8,2,512]{3,1,2,0:T(8,128)(2,1)} %copy.21) | copy-start | bytes 3145732
  148.7 36.6 %copy-start.4 = (bf16[512,2048]{1,0:T(8,128)(2,1)S(1)}, bf16[512,2048]{1,0:T(8,128)(2,1)}, u32[]{:S(2)}) copy-start(bf16[512,2048]{1,0:T(8,128)(2,1)} %wq_ref.5) | copy-start | bytes 6291460
  151.5 1.2 copy-start.9
  181.9 1.1 copy-start.7
  185.3 2.2 copy-start.5
  187.4 1.2 copy-start.8
  188.7 1.9 copy-start.10
  256.4 2.0 copy-start.6
  379.2 2.3 copy-start

commit v3 on v2

--- a/solution.py
+++ b/solution.py
@@ -33,7 +33,7 @@
     return (far // mid * 2 + near // 2) * (2 * mid) + far % mid * 2 + near % 2
 
 
-def middle(data_count, tensor_count):
+def middle_size(data_count, tensor_count):
     spare = int(math.log2(data_count)) - int(math.log2(tensor_count)) - 1
     return 1 << (min(2, spare) - 1)
 
@@ -54,6 +54,17 @@
         targets += [{"dp": join(me, (my_far + s) % far_count, mid)} for s in range(1, far_count)]
     if twin:
         targets += [{"tensor": (tensor_index + s) % tensor_count} for s in range(1, tensor_count)]
+    barrier = pltpu.get_barrier_semaphore()
+    for target in targets:
+        pl.semaphore_signal(barrier, inc=1, device_id=target, device_id_type=MESH)
+    pl.semaphore_wait(barrier, len(targets))
+
+
+def meet_all():
+    data_index, data_count = lax.axis_index("dp"), lax.axis_size("dp")
+    tensor_index, tensor_count = lax.axis_index("tensor"), lax.axis_size("tensor")
+    targets = [{"dp": (data_index + s) % data_count} for s in range(1, data_count)]
+    targets += [{"tensor": (tensor_index + s) % tensor_count} for s in range(1, tensor_count)]
     barrier = pltpu.get_barrier_semaphore()
     for target in targets:
         pl.semaphore_signal(barrier, inc=1, device_id=target, device_id_type=MESH)
@@ -211,9 +222,11 @@
                  vg_ref, gq_ref, gkv_ref, normed, stat_out, stat_in, pw_send, pw_recv, st_send,
                  st_recv, far_send, far_recv, near_send, near_recv, twin_send, twin_recv, w_send,
                  w_recv):
-    blocks, tokens, width = x_ref.shape
+    merge_count, tokens, part_width = x_ref.shape
+    blocks, _, width = normed.shape
     far_count = vg_ref.shape[1]
     rows, wide = pwg_ref.shape[1:]
+    feature = rows // merge_count
     tensor_count = lax.axis_size("tensor")
     me, my_far, tensor_index = here(mid)
     meet(mid)
@@ -236,13 +249,13 @@
     for copy in w_copies[:early]:
         copy.start()
 
-    count = blocks * width
+    count = merge_count * part_width
     total = jnp.zeros((tokens, 1), jnp.float32)
-    for at in range(blocks):
+    for at in range(merge_count):
         total = total + jnp.sum(x_ref[at].astype(jnp.float32), axis=-1, keepdims=True)
     mean = total / count
     spread = jnp.zeros((tokens, 1), jnp.float32)
-    for at in range(blocks):
+    for at in range(merge_count):
         centered = x_ref[at].astype(jnp.float32) - mean
         spread = spread + jnp.sum(centered * centered, axis=-1, keepdims=True)
     stat_out[0] = jnp.broadcast_to(mean, stat_out.shape[1:])
@@ -267,12 +280,18 @@
     average = sum(means) / tensor_count
     variance = sum(s + count * (one - average) * (one - average) for s, one in zip(spreads, means))
     scale = lax.rsqrt(variance / (count * tensor_count) + vision_epsilon)
+    merged = [
+        (x_ref[at].astype(jnp.float32) - average) * scale * gain_ref[pl.ds(at, 1)]
+        + bias_ref[pl.ds(at, 1)]
+        for at in range(merge_count)
+    ]
     far_copies = []
     for at in range(blocks):
-        centered = (x_ref[at].astype(jnp.float32) - average) * scale
-        normed[at] = (centered * gain_ref[pl.ds(at, 1)] + bias_ref[pl.ds(at, 1)]).astype(
-            normed.dtype
-        )
+        pieces = []
+        for block in range(NEAR):
+            start = join(block, at, mid) * feature
+            pieces += [one[:, start : start + feature] for one in merged]
+        normed[at] = jnp.concatenate(pieces, axis=1).astype(normed.dtype)
         goal = tensor_index * blocks + at
         mine = goal == my_far
         copy = remote(
@@ -293,13 +312,24 @@
         copy.start()
     holder = my_far // blocks == tensor_index
 
-    def twin_copy(ahead, step, block):
+    def twin_copy(ahead, mask):
+        block = flip(me, mask)
         return remote(
             vg_ref.at[block],
             vg_ref.at[block],
-            twin_send.at[ahead - 1, step],
-            twin_recv.at[step],
+            twin_send.at[ahead - 1, mask],
+            twin_recv.at[mask],
             {"tensor": (tensor_index + ahead) % tensor_count},
+        )
+
+    def near_copy(bit, mask):
+        block = flip(me, mask)
+        return remote(
+            vg_ref.at[block],
+            vg_ref.at[block],
+            near_send.at[(bit | mask) - 1],
+            near_recv.at[(bit | mask) - 1],
+            {"dp": join(flip(me, bit), my_far, mid)},
         )
 
     @pl.when(holder)
@@ -313,32 +343,20 @@
                 far_recv.at[source],
                 {"dp": join(me, source, mid)},
             ).wait_recv()
-        near_copies, twin_copies = [], []
-        for step in range(1, NEAR):
-            copy = remote(
-                vg_ref.at[me],
-                vg_ref.at[me],
-                near_send.at[step - 1],
-                near_recv.at[step - 1],
-                {"dp": join((me + step) % NEAR, my_far, mid)},
-            )
-            copy.start()
-            near_copies.append(copy)
-        for step in range(NEAR):
-            block = (me + NEAR - step) % NEAR
-            if step:
-                remote(
-                    vg_ref.at[me],
-                    vg_ref.at[block],
-                    near_send.at[step - 1],
-                    near_recv.at[step - 1],
-                    {"dp": join(block, my_far, mid)},
-                ).wait_recv()
+        near_copies = {mask | bit: near_copy(bit, mask) for bit, mask in ((2, 0), (1, 0), (1, 2))}
+        twin_copies = []
+        near_copies[2].start()
+        near_copies[1].start()
+        for mask in (0, 2, 1, 3):
+            if mask:
+                near_copies[mask].wait_recv()
+            if mask == 2:
+                near_copies[3].start()
             for ahead in range(1, tensor_count):
-                copy = twin_copy(ahead, step, block)
+                copy = twin_copy(ahead, mask)
                 copy.start()
                 twin_copies.append(copy)
-        for copy in near_copies + twin_copies:
+        for copy in list(near_copies.values()) + twin_copies:
             copy.wait_send()
 
     def keep(at, carry):
@@ -351,7 +369,7 @@
     @pl.when(jnp.logical_not(holder))
     def _():
         for step in range(NEAR):
-            twin_copy(1, step, (me + NEAR - step) % NEAR).wait_recv()
+            twin_copy(1, step).wait_recv()
 
     for mine, copy in far_copies:
         pl.when(jnp.logical_not(mine))(copy.wait_send)
@@ -362,11 +380,13 @@
 
 
 def front(x, gain, bias, proj, w_query, w_kv, tile, jobs, data_count, tensor_count, mid):
-    blocks, tokens, width = x.shape
+    merge_count, tokens, part_width = x.shape
     far_count = data_count // NEAR
+    blocks = far_count // tensor_count
+    width = merge_count * part_width // blocks
     rows, columns = proj.shape
     vmem = pl.BlockSpec(memory_space=pltpu.VMEM)
-    anywhere = pl.BlockSpec(memory_space=pl.ANY)
+    anywhere = pl.BlockSpec(memory_space=pltpu.HBM)
     dma = pltpu.SemaphoreType.DMA
     return pl.pallas_call(
         functools.partial(front_kernel, mid, tile, jobs),
@@ -402,13 +422,34 @@
     )(x, gain, bias, proj, w_query, w_kv)
 
 
-def project_kernel(mid, tile, vg_ref, pw_ref, o_ref, own, acc, out, held, send, recv):
+def middle_kernel(mid, tile, span, w_tile, jobs, vg_ref, pw_ref, pick_ref, rows_ref, spot_ref, text_ref,
+                  gain_ref, wq_ref, wkv_ref, gq_in, gkv_in, a_ref, gq_ref, gkv_ref, own, acc, out,
+                  held_ref, t_send, t_recv, tiles, got, r_send, r_recv, seq, sums, sums_in,
+                  leaving, st_send, st_recv, near_send, near_recv, twin_send, twin_recv, w_send,
+                  w_recv):
     near, far_count, tokens, width = vg_ref.shape
-    me, my_far, _ = here(mid)
+    _, seq_len, depth = a_ref.shape
     chunks = own.shape[0]
+    data_index, data_count = lax.axis_index("dp"), lax.axis_size("dp")
+    tensor_count = lax.axis_size("tensor")
+    held = depth // tensor_count
+    model_width = text_ref.shape[1] * tensor_count
+    wide = got.shape[3]
+    spots = spot_ref.shape[1]
+    early = seq_len - span
+    me, my_far, tensor_index = here(mid)
+    shift = held // (far_count // tensor_count)
     bits = []
     while 1 << len(bits) < far_count:
         bits.append(1 << len(bits))
+    meet_all()
+    w_copies = weight_copies(
+        mid, w_tile, jobs, (wq_ref, wkv_ref), (gq_ref, gkv_ref), w_send, w_recv
+    )
+    half = [copy for copy, job in zip(w_copies, jobs) if job[0] == far_count // 2]
+    rest = [copy for copy, job in zip(w_copies, jobs) if job[0] != far_count // 2]
+    for copy in half[:1]:
+        copy.start()
 
     def compute(mask, chunk, dst_ref):
         term = jnp.dot(
@@ -418,158 +459,69 @@
         )
         dst_ref[...] = term.astype(dst_ref.dtype)
 
-    meet(mid, near=False, twin=False)
-    sums = []
+    parts = []
     for chunk in range(chunks):
         one = Halving(
             bits, my_far, lambda far: {"dp": join(me, far, mid)}, 32, out.at[chunk],
-            held.at[chunk], acc.at[chunk], own.at[chunk], send.at[chunk], recv.at[chunk],
+            held_ref.at[chunk], acc.at[chunk], own.at[chunk], t_send.at[chunk], t_recv.at[chunk],
         )
         for mask in one.masks(0):
             compute(mask, chunk, out.at[chunk, mask - 1])
         one.start(0)
-        sums.append(one)
-    for chunk, one in enumerate(sums):
+        parts.append(one)
+    for copy in rest:
+        copy.start()
+    for chunk, one in enumerate(parts):
         for mask, slot in one.slot.items():
             compute(mask, chunk, acc.at[chunk, slot])
         compute(0, chunk, own.at[chunk])
-    for stage in range(len(bits)):
-        for one in sums:
-            one.receive(stage)
-    for chunk, one in enumerate(sums):
-        o_ref[:, pl.ds(chunk * tile, tile)] = own[chunk].astype(o_ref.dtype)
-        one.finish()
-
-
-def project(vg, pw, mid):
-    near, far_count, tokens, width = vg.shape
-    columns = pw.shape[1]
-    tile = math.gcd(columns, 512)
-    chunks, rows = columns // tile, near * tokens
-    dma = pltpu.SemaphoreType.DMA
-    return pl.pallas_call(
-        functools.partial(project_kernel, mid, tile),
-        out_shape=jax.ShapeDtypeStruct((rows, columns), vg.dtype),
-        in_specs=[pl.BlockSpec(memory_space=pltpu.VMEM)] * 2,
-        out_specs=pl.BlockSpec(memory_space=pltpu.VMEM),
-        scratch_shapes=[
-            pltpu.VMEM((chunks, rows, tile), jnp.float32),
-            pltpu.VMEM((chunks, far_count // 2 - 1, rows, tile), jnp.float32),
-            pltpu.VMEM((chunks, far_count - 1, rows, tile), vg.dtype),
-            pltpu.VMEM((chunks, far_count - 1, rows, tile), vg.dtype),
-            dma((chunks, far_count - 1)),
-            dma((chunks, far_count - 1)),
-        ],
-        compiler_params=pltpu.CompilerParams(
-            collective_id=1, has_side_effects=True, vmem_limit_bytes=40 << 20
-        ),
-        cost_estimate=pl.CostEstimate(
-            flops=2 * far_count * near * tokens * width * columns,
-            bytes_accessed=80 << 20,
-            transcendentals=0,
-        ),
-    )(vg, pw)
-
-
-def route_kernel(mid, x_ref, o_ref, send, recv, own_sem):
-    size = x_ref.shape[0]
-    data_index = lax.axis_index("dp")
-    me, my_far, _ = here(mid)
-    own = pltpu.make_async_copy(x_ref.at[data_index], o_ref.at[me, my_far], own_sem)
-    own.start()
-    barrier = pltpu.get_barrier_semaphore()
-    for step in range(1, size):
-        pl.semaphore_signal(
-            barrier,
-            inc=1,
-            device_id={"dp": (data_index + step) % size},
-            device_id_type=MESH,
-        )
-    pl.semaphore_wait(barrier, size - 1)
-    copies = []
-    for step in range(1, size):
-        target = (data_index + step) % size
-        copy = remote(
-            x_ref.at[target],
-            o_ref.at[me, my_far],
-            send.at[step - 1],
-            recv.at[step - 1],
-            {"dp": target},
-        )
-        copy.start()
-        copies.append(copy)
-    own.wait()
-    for copy in copies:
-        copy.wait()
-
-
-def route(tiles, mid):
-    size = tiles.shape[0]
-    dma = pltpu.SemaphoreType.DMA
-    return pl.pallas_call(
-        functools.partial(route_kernel, mid),
-        out_shape=jax.ShapeDtypeStruct((NEAR, size // NEAR) + tiles.shape[1:], tiles.dtype),
-        in_specs=[pl.BlockSpec(memory_space=pltpu.VMEM)],
-        out_specs=pl.BlockSpec(memory_space=pltpu.VMEM),
-        scratch_shapes=[dma((size - 1,)), dma((size - 1,)), dma],
-        compiler_params=pltpu.CompilerParams(
-            collective_id=2, has_side_effects=True, vmem_limit_bytes=24 << 20
-        ),
-        cost_estimate=pl.CostEstimate(flops=0, bytes_accessed=40 << 20, transcendentals=0),
-    )(tiles)
-
-
-def sequence_kernel(mid, rows, tile, jobs, spot_ref, text_ref, got_ref, gain_ref, wq_ref,
-                    wkv_ref, gq_in, gkv_in, a_ref, gq_ref, gkv_ref, seq, sums, sums_in, leaving,
-                    st_send, st_recv, near_send, near_recv, twin_send, twin_recv, w_send, w_recv):
-    _, seq_len, depth = a_ref.shape
-    near, _, wide = got_ref.shape
-    tensor_count = lax.axis_size("tensor")
-    held = depth // tensor_count
-    model_width = text_ref.shape[1] * tensor_count
-    me, my_far, tensor_index = here(mid)
-    shift = held // (lax.axis_size("dp") // NEAR // tensor_count)
-    meet(mid)
-    w_copies = weight_copies(
-        mid, tile, jobs, (wq_ref, wkv_ref), (gq_ref, gkv_ref), w_send, w_recv
-    )
-    for copy in w_copies:
-        copy.start()
-
-    def fill(at, carry):
-        window = pl.ds(pl.multiple_of(at * rows, rows), rows)
-        place = lax.broadcasted_iota(jnp.int32, (rows, spot_ref.shape[1]), 0) + at * rows
-        chosen = jnp.where(place == spot_ref[...], 1.0, 0.0)
-        image = jnp.max(chosen, axis=-1, keepdims=True) > 0.5
-        chosen = chosen.astype(jnp.bfloat16)
+
+    rows = math.gcd(early, span)
+
+    def fill(start, image):
+        window = pl.ds(pl.multiple_of(start, rows), rows)
+        place = lax.broadcasted_iota(jnp.int32, (rows, seq_len), 1)
+        chosen = jnp.where(place == rows_ref[window, :], 1.0, 0.0).astype(jnp.bfloat16)
+        if image:
+            slots = lax.broadcasted_iota(jnp.int32, (rows, spots), 0) + (start - early)
+            drawn = jnp.where(slots == spot_ref[...], 1.0, 0.0)
+            is_image = jnp.max(drawn, axis=-1, keepdims=True) > 0.5
+            drawn = drawn.astype(jnp.bfloat16)
         squares = jnp.zeros((rows, 1), jnp.float32)
         for part in range(near):
             lanes = pl.ds(part * wide, wide)
-            drawn = jnp.dot(chosen, got_ref[part], preferred_element_type=jnp.float32)
-            value = jnp.where(image, drawn, text_ref[window, lanes].astype(jnp.float32))
+            value = jnp.dot(chosen, text_ref[:, lanes], preferred_element_type=jnp.float32)
+            if image:
+                tokens_here = got[part].reshape(spots, wide)
+                tile_rows = jnp.dot(drawn, tokens_here, preferred_element_type=jnp.float32)
+                value = jnp.where(is_image, tile_rows, value)
             seq[window, lanes] = value.astype(seq.dtype)
             squares = squares + jnp.sum(value * value, axis=-1, keepdims=True)
         sums[window, :] = jnp.broadcast_to(squares, (rows, sums.shape[1]))
-        return carry
-
-    lax.fori_loop(0, seq_len // rows, fill, 0)
-    stat_copies = []
-    for step in range(1, tensor_count):
-        copy = remote(
-            sums,
-            sums_in.at[step - 1],
-            st_send.at[step - 1],
-            st_recv.at[step - 1],
-            {"tensor": (tensor_index + step) % tensor_count},
-        )
-        copy.start()
-        stat_copies.append(copy)
-    for copy in stat_copies:
-        copy.wait_recv()
-
-    def norm(target, store):
+
+    def share(phase, low, count):
+        window = pl.ds(low, count)
+        copies = []
+        for step in range(1, tensor_count):
+            copy = remote(
+                sums.at[window],
+                sums_in.at[step - 1, window],
+                st_send.at[phase, step - 1],
+                st_recv.at[phase, step - 1],
+                {"tensor": (tensor_index + step) % tensor_count},
+            )
+            copy.start()
+            copies.append(copy)
+        return copies
+
+    def lanes_of(owner):
+        return pl.ds(pl.multiple_of(owner * held, held), held)
+
+    fine = math.gcd(rows, 32)
+
+    def norm(target, low, count, store):
         def one(at, carry):
-            window = pl.ds(pl.multiple_of(at * rows, rows), rows)
+            window = pl.ds(pl.multiple_of(low + at * fine, fine), fine)
             squares = sums[window, :][:, :1]
             for step in range(1, tensor_count):
                 squares = squares + sums_in[step - 1, window, :][:, :1]
@@ -580,94 +532,170 @@
                 store(window, part * shift, value.astype(jnp.bfloat16))
             return carry
 
-        lax.fori_loop(0, seq_len // rows, one, 0)
-
-    def lanes_of(owner):
-        return pl.ds(pl.multiple_of(owner * held, held), held)
-
-    near_copies, twin_copies = [], []
-    for step in range(1, NEAR):
-        target = flip(me, step)
-
-        def leave(window, start, value):
-            leaving[step - 1, window, pl.ds(start, shift)] = value
-
-        norm(target, leave)
-        copy = remote(
-            leaving.at[step - 1],
-            a_ref.at[me, :, lanes_of(tensor_index)],
-            near_send.at[step - 1],
-            near_recv.at[step - 1],
-            {"dp": join(target, my_far, mid)},
-        )
-        copy.start()
-        near_copies.append(copy)
+        lax.fori_loop(0, count // fine, one, 0)
 
     def stay(window, start, value):
         lanes = pl.ds(pl.multiple_of(tensor_index * held + start, shift), shift)
         a_ref[me, window, lanes] = value
 
-    norm(me, stay)
-
-    def twin_copy(ahead, step, owner):
-        block = flip(me, step)
+    def spread(phase, low, count):
+        window = pl.ds(low, count)
+        copies = []
+        for step in range(1, NEAR):
+
+            def leave(window, start, value):
+                leaving[step - 1, window, pl.ds(start, shift)] = value
+
+            norm(flip(me, step), low, count, leave)
+            copy = remote(
+                leaving.at[step - 1, window],
+                a_ref.at[me, window, lanes_of(tensor_index)],
+                near_send.at[phase, step - 1],
+                near_recv.at[phase, step - 1],
+                {"dp": join(flip(me, step), my_far, mid)},
+            )
+            copy.start()
+            copies.append(copy)
+        norm(me, low, count, stay)
+        return copies
+
+    def twin_copy(phase, low, count, ahead, step, owner):
+        block, window = flip(me, step), pl.ds(low, count)
         return remote(
-            a_ref.at[block, :, lanes_of(owner)],
-            a_ref.at[block, :, lanes_of(owner)],
-            twin_send.at[ahead - 1, step],
-            twin_recv.at[ahead - 1, step],
+            a_ref.at[block, window, lanes_of(owner)],
+            a_ref.at[block, window, lanes_of(owner)],
+            twin_send.at[phase, ahead - 1, step],
+            twin_recv.at[phase, ahead - 1, step],
             {"tensor": (tensor_index + ahead) % tensor_count},
         )
 
-    for step in range(NEAR):
-        if step:
-            near_copies[step - 1].wait_recv()
+    def pass_on(phase, low, count, near_copies):
+        copies = []
+        for step in range(NEAR):
+            if step:
+                near_copies[step - 1].wait_recv()
+            for ahead in range(1, tensor_count):
+                copy = twin_copy(phase, low, count, ahead, step, tensor_index)
+                copy.start()
+                copies.append(copy)
+        return copies
+
+    def collect(phase, low, count):
         for ahead in range(1, tensor_count):
-            copy = twin_copy(ahead, step, tensor_index)
-            copy.start()
-            twin_copies.append(copy)
-    for ahead in range(1, tensor_count):
-        for step in range(NEAR):
-            owner = (tensor_index + tensor_count - ahead) % tensor_count
-            twin_copy(ahead, step, owner).wait_recv()
-    for copy in near_copies + twin_copies + stat_copies:
+            for step in range(NEAR):
+                owner = (tensor_index + tensor_count - ahead) % tensor_count
+                twin_copy(phase, low, count, ahead, step, owner).wait_recv()
+
+    for start in range(0, early, rows):
+        fill(start, False)
+    stat_copies = share(0, 0, early)
+    for one in parts:
+        one.receive(0)
+    for copy in stat_copies:
+        copy.wait_recv()
+    near_early = spread(0, 0, early)
+    for stage in range(1, len(bits)):
+        for one in parts:
+            one.receive(stage)
+
+    place = lax.broadcasted_iota(jnp.int32, (pick_ref.shape[0], near * tokens), 1)
+    chosen = jnp.where(place == pick_ref[...], 1.0, 0.0).astype(jnp.bfloat16)
+    for chunk in range(chunks):
+        image = own[chunk].astype(jnp.bfloat16)
+        sorted_rows = jnp.dot(chosen, image, preferred_element_type=jnp.float32)
+        tiles[:, :, pl.ds(chunk * tile, tile)] = sorted_rows.astype(tiles.dtype).reshape(
+            tiles.shape[0], tiles.shape[1], tile
+        )
+    route_copies = []
+    for step in range(1, data_count):
+        target = (data_index + step) % data_count
+        copy = remote(
+            tiles.at[target],
+            got.at[me, my_far],
+            r_send.at[step - 1],
+            r_recv.at[step - 1],
+            {"dp": target},
+        )
+        copy.start()
+        route_copies.append(copy)
+    for copy in half[1:]:
+        copy.start()
+    got[me, my_far] = tiles[data_index]
+    twin_early = pass_on(0, 0, early, near_early)
+    for copy in route_copies:
+        copy.wait_recv()
+    for start in range(early, seq_len, rows):
+        fill(start, True)
+    late_copies = share(1, early, span)
+    for copy in late_copies:
+        copy.wait_recv()
+    near_late = spread(1, early, span)
+    twin_late = pass_on(1, early, span, near_late)
+    collect(0, 0, early)
+    collect(1, early, span)
+    for copy in near_early + near_late + twin_early + twin_late + stat_copies + late_copies:
         copy.wait_send()
+    for copy in route_copies:
+        copy.wait_send()
+    for one in parts:
+        one.finish()
     for copy in w_copies:
         copy.wait()
 
 
-def sequences(spots, text, got, gain, weights, gathered, tile, jobs, tensor_count, mid):
+def middle_part(vg, pw, pick, rows, spots, span, text, gain, weights, gathered, w_tile, jobs, mid):
+    near, far_count, tokens, width = vg.shape
+    columns = pw.shape[1]
+    tensor_count = lax.axis_size("tensor")
+    data_count = lax.axis_size("dp")
+    tile = math.gcd(columns, 512)
+    chunks = columns // tile
     seq_len, part_model = text.shape
     held = part_model // NEAR
+    sent = pick.shape[0] // data_count
     vmem = pl.BlockSpec(memory_space=pltpu.VMEM)
-    anywhere = pl.BlockSpec(memory_space=pl.ANY)
+    anywhere = pl.BlockSpec(memory_space=pltpu.HBM)
     dma = pltpu.SemaphoreType.DMA
     return pl.pallas_call(
-        functools.partial(sequence_kernel, mid, math.gcd(seq_len, 32), tile, jobs),
+        functools.partial(middle_kernel, mid, tile, span, w_tile, jobs),
         out_shape=(jax.ShapeDtypeStruct((NEAR, seq_len, held * tensor_count), text.dtype),)
         + tuple(jax.ShapeDtypeStruct(one.shape, one.dtype) for one in gathered),
-        in_specs=[vmem] * 4 + [anywhere] * 4,
+        in_specs=[vmem] * 7 + [anywhere] * 4,
         out_specs=(vmem, anywhere, anywhere),
-        input_output_aliases={6: 1, 7: 2},
+        input_output_aliases={9: 1, 10: 2},
         scratch_shapes=[
+            pltpu.VMEM((chunks, near * tokens, tile), jnp.float32),
+            pltpu.VMEM((chunks, far_count // 2 - 1, near * tokens, tile), jnp.float32),
+            pltpu.VMEM((chunks, far_count - 1, near * tokens, tile), vg.dtype),
+            pltpu.VMEM((chunks, far_count - 1, near * tokens, tile), vg.dtype),
+            dma((chunks, far_count - 1)),
+            dma((chunks, far_count - 1)),
+            pltpu.VMEM((data_count, sent, columns), vg.dtype),
+            pltpu.VMEM((NEAR, far_count, sent, columns), vg.dtype),
+            dma((data_count - 1,)),
+            dma((data_count - 1,)),
             pltpu.VMEM((seq_len, part_model), text.dtype),
             pltpu.VMEM((seq_len, 128), jnp.float32),
             pltpu.VMEM((tensor_count - 1, seq_len, 128), jnp.float32),
             pltpu.VMEM((NEAR - 1, seq_len, held), text.dtype),
-            dma((tensor_count - 1,)),
-            dma((tensor_count - 1,)),
-            dma((NEAR - 1,)),
-            dma((NEAR - 1,)),
-            dma((tensor_count - 1, NEAR)),
-            dma((tensor_count - 1, NEAR)),
+            dma((2, tensor_count - 1)),
+            dma((2, tensor_count - 1)),
+            dma((2, NEAR - 1)),
+            dma((2, NEAR - 1)),
+            dma((2, tensor_count - 1, NEAR)),
+            dma((2, tensor_count - 1, NEAR)),
             dma((len(jobs),)),
             dma((len(jobs),)),
         ],
         compiler_params=pltpu.CompilerParams(
-            collective_id=3, has_side_effects=True, vmem_limit_bytes=40 << 20
+            collective_id=1, has_side_effects=True, vmem_limit_bytes=48 << 20
         ),
-        cost_estimate=pl.CostEstimate(flops=0, bytes_accessed=100 << 20, transcendentals=0),
-    )(spots, text, got, gain, *weights, *gathered)
+        cost_estimate=pl.CostEstimate(
+            flops=2 * far_count * near * tokens * width * columns,
+            bytes_accessed=100 << 20,
+            transcendentals=0,
+        ),
+    )(vg, pw, pick, rows, spots, text, gain, *weights, *gathered)
 
 
 def product_kernel(mid, tile, jobs, have, a_ref, wq_ref, wkv_ref, gq_ref, gkv_ref, o_ref, w, acc,
@@ -728,13 +756,14 @@
             copy.start()
 
     sums = []
+    third = chunks // 3
 
     def compute(chunk):
         forward(chunk)
         for mask in range(far_count):
             ensure(mask, chunk)
         part = pl.ds(chunk * tile, tile)
-        bits = (1, 2) if chunk % 2 else (2, 1)
+        bits = (2, 1) if chunk % 2 and chunk < 2 * third else (1, 2)
         one = Halving(
             bits, me, lambda near: {"dp": join(near, my_far, mid)}, math.gcd(seq_len, 32),
             out.at[chunk], held.at[chunk], acc.at[chunk], o_ref.at[:, part], send.at[chunk],
@@ -762,7 +791,6 @@
             one.receive(stage)
         done[stage] = max(done[stage], upto)
 
-    third = chunks // 3
     for chunk in range(2 * third):
         compute(chunk)
     reduce(0, third)
@@ -785,7 +813,7 @@
     columns = sum(one.shape[1] for one in weights)
     chunks = columns // tile
     vmem = pl.BlockSpec(memory_space=pltpu.VMEM)
-    anywhere = pl.BlockSpec(memory_space=pl.ANY)
+    anywhere = pl.BlockSpec(memory_space=pltpu.HBM)
     far_count = gathered[0].shape[0]
     dma = pltpu.SemaphoreType.DMA
     return pl.pallas_call(
@@ -805,7 +833,7 @@
             dma((chunks, far_count)),
         ],
         compiler_params=pltpu.CompilerParams(
-            collective_id=4, has_side_effects=True, vmem_limit_bytes=56 << 20
+            collective_id=2, has_side_effects=True, vmem_limit_bytes=56 << 20
         ),
         cost_estimate=pl.CostEstimate(
             flops=2 * NEAR * seq_len * depth * columns,
@@ -815,7 +843,7 @@
     )(a, *weights, *gathered)
 
 
-def attend_kernel(group, q_ref, k_ref, v_ref, cos_ref, sin_ref, o_ref):
+def attend_kernel(group, q_ref, k_ref, v_ref, cos_ref, sin_ref, down_ref, across_ref, o_ref):
     cosine, sine = cos_ref[...], sin_ref[...]
 
     def turn(rows):
@@ -824,24 +852,28 @@
     key_rows = turn(k_ref[...])
     value_rows = v_ref[...].astype(jnp.bfloat16)
     seq_len = key_rows.shape[0]
+    allowed = down_ref[...] >= across_ref[...]
     row_at = lax.broadcasted_iota(jnp.int32, (seq_len, seq_len), 0)
-    column_at = lax.broadcasted_iota(jnp.int32, (seq_len, seq_len), 1)
+    home = jnp.where(row_at == across_ref[...], 1.0, 0.0).astype(jnp.bfloat16)
     for head in range(group):
         part = pl.ds(head * HEAD_WIDTH, HEAD_WIDTH)
         query_rows = turn(q_ref[:, part])
         scores = lax.dot_general(
             query_rows, key_rows, (((1,), (1,)), ((), ())), preferred_element_type=jnp.float32
         ) * HEAD_WIDTH ** (-0.5)
-        scores = jnp.where(row_at >= column_at, scores, -1e30)
+        scores = jnp.where(allowed, scores, -1e30)
         exponentials = jnp.exp(scores - jnp.max(scores, axis=-1, keepdims=True))
         weights = exponentials / jnp.sum(exponentials, axis=-1, keepdims=True)
         context = jnp.dot(
             weights.astype(jnp.bfloat16), value_rows, preferred_element_type=jnp.float32
         )
-        o_ref[:, part] = context.astype(o_ref.dtype)
-
-
-def attend(product, part_query):
+        ordered = jnp.dot(
+            home, context.astype(jnp.bfloat16), preferred_element_type=jnp.float32
+        )
+        o_ref[:, part] = ordered.astype(o_ref.dtype)
+
+
+def attend(product, positions, part_query):
     seq_len, columns = product.shape
     group = QUERY_HEADS // KEY_VALUE_HEADS
     local_kv = part_query // HEAD_WIDTH // group
@@ -849,7 +881,7 @@
     half_width = HEAD_WIDTH // 2
     exponents = jnp.arange(half_width, dtype=jnp.float32) * (2.0 / HEAD_WIDTH)
     frequency = rope_base ** (-exponents)
-    angles = jnp.arange(seq_len, dtype=jnp.float32)[:, None] * frequency[None, :]
+    angles = positions.astype(jnp.float32)[:, None] * frequency[None, :]
     cosine, sine = jnp.cos(angles), jnp.sin(angles)
     cosine = jnp.concatenate([cosine, cosine], axis=1)
     sine = jnp.concatenate([-sine, sine], axis=1)
@@ -864,10 +896,12 @@
             pl.BlockSpec((seq_len, HEAD_WIDTH), lambda g: (0, key_at + local_kv + g)),
             table,
             table,
+            pl.BlockSpec((seq_len, 1), lambda g: (0, 0)),
+            pl.BlockSpec((1, seq_len), lambda g: (0, 0)),
         ],
         out_specs=pl.BlockSpec((seq_len, group * HEAD_WIDTH), lambda g: (0, g)),
         compiler_params=pltpu.CompilerParams(vmem_limit_bytes=24 << 20),
-    )(product, product, product, cosine, sine)
+    )(product, product, product, cosine, sine, positions[:, None], positions[None, :])
 
 
 def per_device(
@@ -890,7 +924,7 @@
     feature = proj_weight.shape[0]
     part_model = proj_weight.shape[2]
     tokens = tile_rows * tile_tok
-    mid = middle(data_count, tensor_count)
+    mid = middle_size(data_count, tensor_count)
     far_count = data_count // NEAR
     far_here = far_count // tensor_count
     depth = w_query.shape[0]
@@ -899,24 +933,14 @@
     chunks = sum(one.shape[1] for one in weights) // tile
     plan, have = gather_plan(far_count, chunks)
 
-    tops = far_here // mid
-    split = (tops, 2, mid, 2, feature)
-
-    def arranged(rows):
-        parts = rows.reshape(rows.shape[:-1] + split)
-        lead = rows.ndim - 2
-        order = (lead + 1, lead + 3) + tuple(range(lead)) + (lead + 2, lead + 4, lead, lead + 5)
-        return parts.transpose(order).reshape((far_here,) + rows.shape[:lead] + (-1,))
-
     start = tensor_index * part_width
-    gain = arranged(lax.dynamic_slice_in_dim(ln_gain, start, part_width, 1))
-    bias = arranged(lax.dynamic_slice_in_dim(ln_bias, start, part_width, 1))
-    rows_in = arranged(vis_rows.reshape(tokens, merge_count, part_width))
+    gain = lax.dynamic_slice_in_dim(ln_gain, start, part_width, 1)
+    bias = lax.dynamic_slice_in_dim(ln_bias, start, part_width, 1)
+    rows_in = vis_rows.reshape(tokens, merge_count, part_width).transpose(1, 0, 2)
     proj = proj_weight.transpose(1, 0, 2).reshape(merge_count * feature, part_model)
     proj, normed, *gathered = front(
         rows_in, gain, bias, proj, *weights, tile, plan["front"], data_count, tensor_count, mid
     )
-    image = project(normed, proj.reshape(-1, proj.shape[2]), mid)
 
     max_tiles = 2 * tile_rows
     tile_ends = jnp.cumsum(tile_counts)
@@ -926,9 +950,8 @@
     ranks = (sources[None, :] - tile_firsts[:, None]) % data_count
     taken = jnp.clip((tile_firsts[:, None] + ranks) // data_count, 0, tile_rows - 1)
     taken = taken + jnp.arange(NEAR, dtype=jnp.int32)[None, :] * tile_rows
-    image = image.reshape(NEAR * tile_rows, tile_tok, image.shape[1])
-    routed = image[taken].reshape(data_count, NEAR * tile_tok, image.shape[2])
-    received = route(routed, mid).reshape(NEAR, data_count * tile_tok, image.shape[2])
+    token_at = jnp.arange(tile_tok, dtype=jnp.int32)
+    pick = (taken.reshape(-1, 1) * tile_tok + token_at[None, :]).reshape(-1, 1)
 
     is_mine = jnp.arange(data_count, dtype=jnp.int32) == data_index
     my_first = jnp.sum(jnp.where(is_mine, tile_firsts, 0))
@@ -936,16 +959,22 @@
     far_ids = jnp.arange(far_count, dtype=jnp.int32)[:, None]
     tile_ids = join(jnp.arange(NEAR, dtype=jnp.int32)[None, :], far_ids, mid).reshape(-1)
     order = (tile_ids - my_first) % data_count
-    spots = image_offsets[0] + order * tile_tok
-    spots = spots[:, None] + jnp.arange(tile_tok, dtype=jnp.int32)[None, :]
+    spots = order[:, None] * tile_tok + token_at[None, :]
     spots = jnp.where((order < my_count)[:, None], spots, -1).reshape(1, -1)
+
+    seq_len = text_rows.shape[1]
+    image_span = max_tiles * tile_tok
+    offset = image_offsets[0]
+    outside = jnp.arange(seq_len - image_span, dtype=jnp.int32)
+    outside = jnp.where(outside < offset, outside, outside + image_span)
+    positions = jnp.concatenate([outside, offset + jnp.arange(image_span, dtype=jnp.int32)])
     gain = lax.dynamic_slice_in_dim(attn_gain, tensor_index * part_model, part_model, 0)
-    sequence, *gathered = sequences(
-        spots, text_rows[0], received, gain[None, :], weights, gathered, tile,
-        plan["sequence"], tensor_count, mid,
+    sequence, *gathered = middle_part(
+        normed, proj.reshape(-1, proj.shape[2]), pick, positions[:, None], spots, image_span,
+        text_rows[0], gain[None, :], weights, gathered, tile, plan["sequence"], mid,
     )
     product = product_blocks(sequence, weights, gathered, tile, plan["product"], have, mid)
-    context = attend(product, w_query.shape[1])
+    context = attend(product, positions, w_query.shape[1])
     return context[None]
 
 

time: 393 us -> 369 us (0.939)
  local copies, waits for them, and re-layouts: 35.6 us -> 14.1 us
    pallas_call x3 -> x1, Pallas kernels: 133 us -> 112 us  [middle_part(): pl.pallas_call(functools.partial(middle_kernel, mid, tile, span, w_tile,...]
    pallas_call x1, Pallas kernels: 120 us -> 134 us  [product_blocks(): pl.pallas_call(functools.partial(product_kernel, mid, tile, jobs, have),...]
    unnamed x29 -> x16, local copies, waits for them, and re-layouts: 19 us -> 7.27 us
    another operation x3 -> x1, local copies, waits for them, and re-layouts: 5.82 us -> 0.73 us  [the longest x2 5.09 us: arranged(): parts = rows.reshape(rows.shape[:-1] + split)]
    pallas_call x1, Pallas kernels: 8.93 us -> 13.6 us  [attend(): pl.pallas_call(functools.partial(attend_kernel, group), grid=(local_kv,),...]
where the time goes in v3:
time: 369 us
  Pallas kernels  350 us (95%)
  local copies, waits for them, and re-layouts  14.1 us (4%)
  other arithmetic  3.89 us (1%)
    pallas_call x1, Pallas kernels, product_blocks(): pl.pallas_call(functools.partial(product_kernel, mid, tile, jobs, have),...  134 us
    pallas_call x1, Pallas kernels, middle_part(): pl.pallas_call(functools.partial(middle_kernel, mid, tile, span, w_tile,...  112 us
    pallas_call x1, Pallas kernels, front(): pl.pallas_call(functools.partial(front_kernel, mid, tile, jobs), out_shap...  89.6 us
    pallas_call x1, Pallas kernels, attend(): pl.pallas_call(functools.partial(attend_kernel, group), grid=(local_kv,),...  13.6 us

profile of v3, /device:TPU:10, one launch (start us, length us, event | category | flops | bytes accessed | tf_op | source)
XLA Modules:
  0.0 368.7 jit_solution(12886421081139935839)
XLA Ops:
  0.0 0.7 copy.18
  0.8 0.1 reduce
  0.9 1.3 fusion.2
  2.2 0.7 add_subtract_fusion
  2.9 0.1 reshape.355
  3.0 0.6 broadcast_compare_fusion
  3.6 0.1 add_select_fusion
  3.7 0.1 select_n.159.spot_ref
  3.8 0.1 sub.66
  3.9 0.1 add.271
  3.9 0.1 add.272
  4.0 0.1 add.285
  4.2 0.1 iota_add_fusion
  4.2 0.1 add.308.pick_ref
  4.4 0.8 constant_dynamic-slice_fusion
  5.2 1.5 copy.22
  6.7 0.0 copy-start.1
  6.7 0.0 copy-start.5
  6.7 0.0 copy-start.2
  6.7 4.6 %copy.17 = bf16[2,200,4096]{2,1,0:T(8,128)(2,1)S(1)} copy(bf16[2,200,4096]{2,0,1:T(2,128)(2,1)} %bitcast.24) | data formatting | bytes 6553600 | tf_op jit(solution)/shard_map/transpose | solution.py:940
  11.3 0.0 copy-start.6
  11.4 89.6 %shard_map.100 = (bf16[4,400,1024]{2,1,0:T(8,128)(2,1)S(1)}, bf16[4,4,64,1600]{3,2,1,0:T(8,128)(2,1)S(1)}, bf16[4,512,2048]{2,1,0:T(8,128)(2,1)}, bf16[4,512,1024]{2,1,0:T(8,128)(2,1)}) custom-call(bf16[2,64,1600]{2,1,0:T(8,128)(2,1)S(1)} %bitcast.22, f32[2,1600]{1,0:T(2,128)S(1)} %get-tuple-element.34.gain_ref, f32[2,1600]{1,0:T(2,128)S(1)} %get-tuple-element.33.bias_ref, ...), custom_call_target="tpu_custom_call" | custom-call | bytes 83886080 | tf_op jit(solution)/shard_map/pallas_call | solution.py:391
  101.0 1.7 copy-done.3
  102.7 1.7 copy-done.4
  104.4 0.0 copy-done.6
  105.1 0.1 broadcast_in_dim.49.rows_ref.down_ref
  105.2 112.2 %shard_map.101 = (bf16[4,384,2048]{2,1,0:T(8,128)(2,1)}, bf16[4,512,2048]{2,1,0:T(8,128)(2,1)}, bf16[4,512,1024]{2,1,0:T(8,128)(2,1)}) custom-call(bf16[4,4,64,1600]{3,2,1,0:T(8,128)(2,1)} %copy-done.3, bf16[1600,1024]{1,0:T(8,128)(2,1)} %bitcast.21, s32[512,1]{1,0:T(8,128)S(1)} %add.308.pick_ref, ...), custom_call_target="tpu_custom_call", output_to_operand_aliasing={{1}: (9, {}), {2}: (10, {})} | custom-call | flops 3355443200 | bytes 104857600 | tf_op jit(solution)/shard_map/pallas_call | solution.py:659
  217.4 134.4 %shard_map.102.q_ref.k_ref.v_ref = f32[384,3072]{1,0:T(8,128)} custom-call(bf16[4,384,2048]{2,1,0:T(8,128)(2,1)} %get-tuple-element.16.a_ref, bf16[512,2048]{1,0:T(8,128)(2,1)} %wq_ref.5, bf16[512,1024]{1,0:T(8,128)(2,1)} %bitcast.20, bf16[4,512,2048]{2,1,0:T(8,128)(2,1)} %get-tuple-element.17.gq_ref, bf16[4,512,1024]{2,1,0:T(8,128)(2,1)} %get-tuple-element.18.gkv_ref), custom_call_target="tpu_custom_call" | custom-call | flops 19327352832 | bytes 209715200 | tf_op jit(solution)/shard_map/pallas_call | solution.py:819
  351.9 0.8 fusion
  352.6 0.2 pad_maximum_fusion
  352.8 2.3 copy-done
  355.2 13.6 %shard_map.103 = bf16[384,2048]{1,0:T(8,128)(2,1)} custom-call(f32[384,3072]{1,0:T(8,128)S(1)} %copy-done, f32[384,3072]{1,0:T(8,128)S(1)} %copy-done, f32[384,3072]{1,0:T(8,128)S(1)} %copy-done, f32[384,128]{1,0:T(8,128)S(1)} %get-tuple-element.35.cos_ref, f32[384,128]{1,0:T(8,128)S(1)} %get-tuple-element.36.sin_ref, ...), custom_call_target="tpu_custom_call" | custom-call | tf_op jit(solution)/shard_map/pallas_call | solution.py:889
  (22 shorter events, 0.2 us)
Async XLA Ops:
  6.7 98.5 %copy-start.1 = (bf16[64,8,2,512]{3,1,2,0:T(8,128)(2,1)}, bf16[64,8,2,512]{3,1,2,0:T(8,128)(2,1)S(1)}, u32[]{:S(2)}) copy-start(bf16[64,8,2,512]{3,1,2,0:T(8,128)(2,1)S(1)} %copy.22) | copy-start | bytes 3145732
  6.7 4.6 %copy-start.5 = (bf16[8,8,2,1600]{3,2,1,0:T(2,128)(2,1)S(1)}, bf16[8,8,2,1600]{3,2,1,0:T(2,128)(2,1)}, u32[]{:S(2)}) copy-start(bf16[8,8,2,1600]{3,2,1,0:T(2,128)(2,1)} %param.10) | copy-start | bytes 1228804
  6.7 4.6 %copy-start.2 = (bf16[512,2048]{1,0:T(8,128)(2,1)S(1)}, bf16[512,2048]{1,0:T(8,128)(2,1)}, u32[]{:S(2)}) copy-start(bf16[512,2048]{1,0:T(8,128)(2,1)} %wq_ref.5) | copy-start | bytes 6291460
  11.3 93.1 %copy-start.6 = (f32[8192]{0:T(1024)S(1)}, f32[8192]{0:T(1024)}, u32[]{:S(2)}) copy-start(f32[8192]{0:T(1024)} %param.15) | copy-start | bytes 98308
  101.0 1.7 copy-start.3
  102.7 1.7 copy-start.4
  352.8 2.3 copy-start

commit v4 on v3

--- a/solution.py
+++ b/solution.py
@@ -106,20 +106,17 @@
     items = gather_items(far_count)
     plan = {"front": [], "sequence": [], "product": []}
     have = {chunk: {0} for chunk in range(chunks)}
-    for name, first, others in (
-        ("front", range(third), range(2 * third)),
-        ("sequence", range(third, 2 * third), range(2 * third, chunks)),
-    ):
-        held = {chunk: set(masks) for chunk, masks in have.items()}
-        done = [job for jobs in plan.values() for job in jobs]
-        for chunk in range(chunks):
-            for bit, mask in items:
-                wanted = (chunk in first) if bit == high else (chunk in others)
-                if mask:
-                    wanted = name == "sequence" and chunk < third and mask in held[chunk]
-                if wanted and (bit, mask, chunk) not in done:
-                    plan[name].append((bit, mask, chunk))
-                    have[chunk].add(bit | mask)
+    plan["front"] = [(high, 0, chunk) for chunk in range(third)]
+    plan["sequence"] = [(high, 0, chunk) for chunk in range(third, 2 * third)]
+    plan["sequence"] += [
+        (bit, 0, chunk) for bit, mask in items if not mask and bit != high
+        for chunk in range(chunks)
+    ]
+    plan["sequence"] += [
+        (bit, mask, chunk) for bit, mask in items if mask == high for chunk in range(third)
+    ]
+    for bit, mask, chunk in plan["front"] + plan["sequence"]:
+        have[chunk].add(bit | mask)
     done = plan["front"] + plan["sequence"]
     for chunk in range(chunks):
         plan["product"] += [
@@ -218,7 +215,7 @@
             copy.wait_send()
 
 
-def front_kernel(mid, tile, jobs, x_ref, gain_ref, bias_ref, pw_ref, wq_ref, wkv_ref, pwg_ref,
+def front_kernel(mid, w_mid, tile, jobs, x_ref, gain_ref, bias_ref, pw_ref, wq_ref, wkv_ref, pwg_ref,
                  vg_ref, gq_ref, gkv_ref, normed, stat_out, stat_in, pw_send, pw_recv, st_send,
                  st_recv, far_send, far_recv, near_send, near_recv, twin_send, twin_recv, w_send,
                  w_recv):
@@ -229,7 +226,7 @@
     feature = rows // merge_count
     tensor_count = lax.axis_size("tensor")
     me, my_far, tensor_index = here(mid)
-    meet(mid)
+    meet_all()
     pw_copies = []
     for step in range(1, NEAR):
         target = (me + step) % NEAR
@@ -243,9 +240,9 @@
         copy.start()
         pw_copies.append(copy)
     w_copies = weight_copies(
-        mid, tile, jobs, (wq_ref, wkv_ref), (gq_ref, gkv_ref), w_send, w_recv
+        w_mid, tile, jobs, (wq_ref, wkv_ref), (gq_ref, gkv_ref), w_send, w_recv
     )
-    early = len(w_copies) // 3
+    early = 1
     for copy in w_copies[:early]:
         copy.start()
 
@@ -379,7 +376,7 @@
         copy.wait()
 
 
-def front(x, gain, bias, proj, w_query, w_kv, tile, jobs, data_count, tensor_count, mid):
+def front(x, gain, bias, proj, w_query, w_kv, tile, jobs, data_count, tensor_count, mid, w_mid):
     merge_count, tokens, part_width = x.shape
     far_count = data_count // NEAR
     blocks = far_count // tensor_count
@@ -389,7 +386,7 @@
     anywhere = pl.BlockSpec(memory_space=pltpu.HBM)
     dma = pltpu.SemaphoreType.DMA
     return pl.pallas_call(
-        functools.partial(front_kernel, mid, tile, jobs),
+        functools.partial(front_kernel, mid, w_mid, tile, jobs),
         out_shape=(
             jax.ShapeDtypeStruct((NEAR, rows, columns // NEAR), proj.dtype),
             jax.ShapeDtypeStruct((NEAR, far_count, tokens, width), x.dtype),
@@ -422,7 +419,7 @@
     )(x, gain, bias, proj, w_query, w_kv)
 
 
-def middle_kernel(mid, tile, span, w_tile, jobs, vg_ref, pw_ref, pick_ref, rows_ref, spot_ref, text_ref,
+def middle_kernel(mid, t_mid, tile, span, w_tile, jobs, vg_ref, pw_ref, pick_ref, rows_ref, spot_ref, text_ref,
                   gain_ref, wq_ref, wkv_ref, gq_in, gkv_in, a_ref, gq_ref, gkv_ref, own, acc, out,
                   held_ref, t_send, t_recv, tiles, got, r_send, r_recv, seq, sums, sums_in,
                   leaving, st_send, st_recv, near_send, near_recv, twin_send, twin_recv, w_send,
@@ -438,6 +435,7 @@
     spots = spot_ref.shape[1]
     early = seq_len - span
     me, my_far, tensor_index = here(mid)
+    t_me, t_far, _ = here(t_mid)
     shift = held // (far_count // tensor_count)
     bits = []
     while 1 << len(bits) < far_count:
@@ -453,7 +451,7 @@
 
     def compute(mask, chunk, dst_ref):
         term = jnp.dot(
-            vg_ref[:, flip(my_far, mask)].reshape(near * tokens, width),
+            vg_ref[:, flip(t_far, mask)].reshape(near * tokens, width),
             pw_ref[:, pl.ds(chunk * tile, tile)],
             preferred_element_type=jnp.float32,
         )
@@ -462,14 +460,14 @@
     parts = []
     for chunk in range(chunks):
         one = Halving(
-            bits, my_far, lambda far: {"dp": join(me, far, mid)}, 32, out.at[chunk],
+            bits, t_far, lambda far: {"dp": join(t_me, far, t_mid)}, 32, out.at[chunk],
             held_ref.at[chunk], acc.at[chunk], own.at[chunk], t_send.at[chunk], t_recv.at[chunk],
         )
         for mask in one.masks(0):
             compute(mask, chunk, out.at[chunk, mask - 1])
         one.start(0)
         parts.append(one)
-    for copy in rest:
+    for copy in rest[:7]:
         copy.start()
     for chunk, one in enumerate(parts):
         for mask, slot in one.slot.items():
@@ -611,16 +609,16 @@
         target = (data_index + step) % data_count
         copy = remote(
             tiles.at[target],
-            got.at[me, my_far],
+            got.at[t_me, t_far],
             r_send.at[step - 1],
             r_recv.at[step - 1],
             {"dp": target},
         )
         copy.start()
         route_copies.append(copy)
-    for copy in half[1:]:
+    for copy in half[1:] + rest[7:]:
         copy.start()
-    got[me, my_far] = tiles[data_index]
+    got[t_me, t_far] = tiles[data_index]
     twin_early = pass_on(0, 0, early, near_early)
     for copy in route_copies:
         copy.wait_recv()
@@ -643,7 +641,7 @@
         copy.wait()
 
 
-def middle_part(vg, pw, pick, rows, spots, span, text, gain, weights, gathered, w_tile, jobs, mid):
+def middle_part(vg, pw, pick, rows, spots, span, text, gain, weights, gathered, w_tile, jobs, mid, t_mid):
     near, far_count, tokens, width = vg.shape
     columns = pw.shape[1]
     tensor_count = lax.axis_size("tensor")
@@ -657,7 +655,7 @@
     anywhere = pl.BlockSpec(memory_space=pltpu.HBM)
     dma = pltpu.SemaphoreType.DMA
     return pl.pallas_call(
-        functools.partial(middle_kernel, mid, tile, span, w_tile, jobs),
+        functools.partial(middle_kernel, mid, t_mid, tile, span, w_tile, jobs),
         out_shape=(jax.ShapeDtypeStruct((NEAR, seq_len, held * tensor_count), text.dtype),)
         + tuple(jax.ShapeDtypeStruct(one.shape, one.dtype) for one in gathered),
         in_specs=[vmem] * 7 + [anywhere] * 4,
@@ -763,7 +761,7 @@
         for mask in range(far_count):
             ensure(mask, chunk)
         part = pl.ds(chunk * tile, tile)
-        bits = (2, 1) if chunk % 2 and chunk < 2 * third else (1, 2)
+        bits = (2, 1) if chunk % 3 == 1 else (1, 2)
         one = Halving(
             bits, me, lambda near: {"dp": join(near, my_far, mid)}, math.gcd(seq_len, 32),
             out.at[chunk], held.at[chunk], acc.at[chunk], o_ref.at[:, part], send.at[chunk],
@@ -855,6 +853,7 @@
     allowed = down_ref[...] >= across_ref[...]
     row_at = lax.broadcasted_iota(jnp.int32, (seq_len, seq_len), 0)
     home = jnp.where(row_at == across_ref[...], 1.0, 0.0).astype(jnp.bfloat16)
+    contexts = []
     for head in range(group):
         part = pl.ds(head * HEAD_WIDTH, HEAD_WIDTH)
         query_rows = turn(q_ref[:, part])
@@ -867,10 +866,11 @@
         context = jnp.dot(
             weights.astype(jnp.bfloat16), value_rows, preferred_element_type=jnp.float32
         )
-        ordered = jnp.dot(
-            home, context.astype(jnp.bfloat16), preferred_element_type=jnp.float32
-        )
-        o_ref[:, part] = ordered.astype(o_ref.dtype)
+        contexts.append(context.astype(jnp.bfloat16))
+    ordered = jnp.dot(
+        home, jnp.concatenate(contexts, axis=1), preferred_element_type=jnp.float32
+    )
+    o_ref[...] = ordered.astype(o_ref.dtype)
 
 
 def attend(product, positions, part_query):
@@ -925,11 +925,11 @@
     part_model = proj_weight.shape[2]
     tokens = tile_rows * tile_tok
     mid = middle_size(data_count, tensor_count)
+    t_mid = 1
     far_count = data_count // NEAR
-    far_here = far_count // tensor_count
     depth = w_query.shape[0]
     weights = (w_query, key_value_weight.reshape(depth, -1))
-    tile = math.gcd(512, *(one.shape[1] for one in weights))
+    tile = math.gcd(256, *(one.shape[1] for one in weights))
     chunks = sum(one.shape[1] for one in weights) // tile
     plan, have = gather_plan(far_count, chunks)
 
@@ -939,14 +939,15 @@
     rows_in = vis_rows.reshape(tokens, merge_count, part_width).transpose(1, 0, 2)
     proj = proj_weight.transpose(1, 0, 2).reshape(merge_count * feature, part_model)
     proj, normed, *gathered = front(
-        rows_in, gain, bias, proj, *weights, tile, plan["front"], data_count, tensor_count, mid
+        rows_in, gain, bias, proj, *weights, tile, plan["front"], data_count, tensor_count,
+        t_mid, mid,
     )
 
     max_tiles = 2 * tile_rows
     tile_ends = jnp.cumsum(tile_counts)
     tile_firsts = tile_ends - tile_counts
-    far_index = far_of(data_index, mid)
-    sources = join(jnp.arange(NEAR, dtype=jnp.int32), far_index, mid)
+    far_index = far_of(data_index, t_mid)
+    sources = join(jnp.arange(NEAR, dtype=jnp.int32), far_index, t_mid)
     ranks = (sources[None, :] - tile_firsts[:, None]) % data_count
     taken = jnp.clip((tile_firsts[:, None] + ranks) // data_count, 0, tile_rows - 1)
     taken = taken + jnp.arange(NEAR, dtype=jnp.int32)[None, :] * tile_rows
@@ -957,7 +958,7 @@
     my_first = jnp.sum(jnp.where(is_mine, tile_firsts, 0))
     my_count = jnp.sum(jnp.where(is_mine, tile_counts, 0))
     far_ids = jnp.arange(far_count, dtype=jnp.int32)[:, None]
-    tile_ids = join(jnp.arange(NEAR, dtype=jnp.int32)[None, :], far_ids, mid).reshape(-1)
+    tile_ids = join(jnp.arange(NEAR, dtype=jnp.int32)[None, :], far_ids, t_mid).reshape(-1)
     order = (tile_ids - my_first) % data_count
     spots = order[:, None] * tile_tok + token_at[None, :]
     spots = jnp.where((order < my_count)[:, None], spots, -1).reshape(1, -1)
@@ -972,6 +973,7 @@
     sequence, *gathered = middle_part(
         normed, proj.reshape(-1, proj.shape[2]), pick, positions[:, None], spots, image_span,
         text_rows[0], gain[None, :], weights, gathered, tile, plan["sequence"], mid,
+        t_mid,
     )
     product = product_blocks(sequence, weights, gathered, tile, plan["product"], have, mid)
     context = attend(product, positions, w_query.shape[1])

time: 369 us -> 348 us (0.943)
  Pallas kernels: 350 us -> 329 us
    pallas_call x1, Pallas kernels: 134 us -> 120 us  [product_blocks(): pl.pallas_call(functools.partial(product_kernel, mid, tile, jobs, have),...]
    pallas_call x2, Pallas kernels: 202 us -> 198 us  [the longest x1 125 us: middle_part(): pl.pallas_call(functools.partial(middle_kernel, mid, t_mid, tile, span, w...]
where the time goes in v4:
time: 348 us
  Pallas kernels  329 us (95%)
  local copies, waits for them, and re-layouts  14.1 us (4%)
  other arithmetic  3.97 us (1%)
    pallas_call x1, Pallas kernels, middle_part(): pl.pallas_call(functools.partial(middle_kernel, mid, t_mid, tile, span, w...  125 us
    pallas_call x1, Pallas kernels, product_blocks(): pl.pallas_call(functools.partial(product_kernel, mid, tile, jobs, have),...  120 us
    pallas_call x1, Pallas kernels, front(): pl.pallas_call(functools.partial(front_kernel, mid, w_mid, tile, jobs), o...  72.5 us
    pallas_call x1, Pallas kernels, attend(): pl.pallas_call(functools.partial(attend_kernel, group), grid=(local_kv,),...  11.7 us
    unnamed x16, local copies, waits for them, and re-layouts  7.28 us

profile of v4, /device:TPU:10, one launch (start us, length us, event | category | flops | bytes accessed | tf_op | source)
XLA Modules:
  0.0 347.8 jit_solution(16713519183317274676)
XLA Ops:
  0.0 0.1 sub.63
  0.1 0.7 copy.18
  0.9 0.1 reduce
  1.0 1.3 fusion.2
  2.3 0.1 add.238
  2.4 0.1 add.239
  2.5 0.1 add.247
  2.6 0.1 iota_add_fusion
  2.7 0.1 add.267.pick_ref
  2.8 0.7 add_subtract_fusion
  3.6 0.1 sub.68
  3.6 0.6 broadcast_compare_fusion
  4.3 0.1 add_select_fusion
  4.4 0.1 select_n.148.spot_ref
  4.5 0.8 constant_dynamic-slice_fusion
  5.3 1.5 copy.22
  6.8 0.0 copy-start.1
  6.8 0.0 copy-start.5
  6.8 0.0 copy-start.2
  6.8 4.6 %copy.17 = bf16[2,200,4096]{2,1,0:T(8,128)(2,1)S(1)} copy(bf16[2,200,4096]{2,0,1:T(2,128)(2,1)} %bitcast.24) | data formatting | bytes 6553600 | tf_op jit(solution)/shard_map/transpose | solution.py:940
  11.4 0.0 copy-start.6
  11.4 72.5 %shard_map.100 = (bf16[4,400,1024]{2,1,0:T(8,128)(2,1)S(1)}, bf16[4,4,64,1600]{3,2,1,0:T(8,128)(2,1)S(1)}, bf16[4,512,2048]{2,1,0:T(8,128)(2,1)}, bf16[4,512,1024]{2,1,0:T(8,128)(2,1)}) custom-call(bf16[2,64,1600]{2,1,0:T(8,128)(2,1)S(1)} %bitcast.22, f32[2,1600]{1,0:T(2,128)S(1)} %get-tuple-element.32.gain_ref, f32[2,1600]{1,0:T(2,128)S(1)} %get-tuple-element.31.bias_ref, ...), custom_call_target="tpu_custom_call" | custom-call | bytes 83886080 | tf_op jit(solution)/shard_map/pallas_call | solution.py:388
  83.9 0.0 copy-start.3
  83.9 1.7 copy-done.3
  85.6 1.7 copy-done.4
  88.0 0.1 broadcast_in_dim.49.rows_ref.down_ref
  88.1 125.1 %shard_map.101 = (bf16[4,384,2048]{2,1,0:T(8,128)(2,1)}, bf16[4,512,2048]{2,1,0:T(8,128)(2,1)}, bf16[4,512,1024]{2,1,0:T(8,128)(2,1)}) custom-call(bf16[4,4,64,1600]{3,2,1,0:T(8,128)(2,1)} %copy-done.3, bf16[1600,1024]{1,0:T(8,128)(2,1)} %bitcast.21, s32[512,1]{1,0:T(8,128)S(1)} %add.267.pick_ref, ...), custom_call_target="tpu_custom_call", output_to_operand_aliasing={{1}: (9, {}), {2}: (10, {})} | custom-call | flops 3355443200 | bytes 104857600 | tf_op jit(solution)/shard_map/pallas_call | solution.py:657
  213.3 119.6 %shard_map.102.q_ref.k_ref.v_ref = f32[384,3072]{1,0:T(8,128)} custom-call(bf16[4,384,2048]{2,1,0:T(8,128)(2,1)} %get-tuple-element.16.a_ref, bf16[512,2048]{1,0:T(8,128)(2,1)} %wq_ref.5, bf16[512,1024]{1,0:T(8,128)(2,1)} %bitcast.20, bf16[4,512,2048]{2,1,0:T(8,128)(2,1)} %get-tuple-element.17.gq_ref, bf16[4,512,1024]{2,1,0:T(8,128)(2,1)} %get-tuple-element.18.gkv_ref), custom_call_target="tpu_custom_call" | custom-call | flops 19327352832 | bytes 209715200 | tf_op jit(solution)/shard_map/pallas_call | solution.py:817
  332.9 0.8 fusion
  333.7 0.2 pad_maximum_fusion
  333.9 2.3 copy-done
  336.2 11.7 %shard_map.103 = bf16[384,2048]{1,0:T(8,128)(2,1)} custom-call(f32[384,3072]{1,0:T(8,128)S(1)} %copy-done, f32[384,3072]{1,0:T(8,128)S(1)} %copy-done, f32[384,3072]{1,0:T(8,128)S(1)} %copy-done, f32[384,128]{1,0:T(8,128)S(1)} %get-tuple-element.33.cos_ref, f32[384,128]{1,0:T(8,128)S(1)} %get-tuple-element.34.sin_ref, ...), custom_call_target="tpu_custom_call" | custom-call | tf_op jit(solution)/shard_map/pallas_call | solution.py:889
  (22 shorter events, 0.2 us)
Async XLA Ops:
  6.8 81.4 %copy-start.1 = (bf16[64,8,2,512]{3,1,2,0:T(8,128)(2,1)}, bf16[64,8,2,512]{3,1,2,0:T(8,128)(2,1)S(1)}, u32[]{:S(2)}) copy-start(bf16[64,8,2,512]{3,1,2,0:T(8,128)(2,1)S(1)} %copy.22) | copy-start | bytes 3145732
  6.8 4.6 %copy-start.5 = (bf16[8,8,2,1600]{3,2,1,0:T(2,128)(2,1)S(1)}, bf16[8,8,2,1600]{3,2,1,0:T(2,128)(2,1)}, u32[]{:S(2)}) copy-start(bf16[8,8,2,1600]{3,2,1,0:T(2,128)(2,1)} %param.10) | copy-start | bytes 1228804
  6.8 4.6 %copy-start.2 = (bf16[512,2048]{1,0:T(8,128)(2,1)S(1)}, bf16[512,2048]{1,0:T(8,128)(2,1)}, u32[]{:S(2)}) copy-start(bf16[512,2048]{1,0:T(8,128)(2,1)} %wq_ref.5) | copy-start | bytes 6291460
  11.4 75.9 %copy-start.6 = (f32[8192]{0:T(1024)S(1)}, f32[8192]{0:T(1024)}, u32[]{:S(2)}) copy-start(f32[8192]{0:T(1024)} %param.15) | copy-start | bytes 98308
  83.9 1.7 copy-start.3
  85.6 1.7 copy-start.4
  333.8 2.3 copy-start

commit v5 on v4

--- a/solution.py
+++ b/solution.py
@@ -696,8 +696,9 @@
     )(vg, pw, pick, rows, spots, text, gain, *weights, *gathered)
 
 
-def product_kernel(mid, tile, jobs, have, a_ref, wq_ref, wkv_ref, gq_ref, gkv_ref, o_ref, w, acc,
-                   out, held, send, recv, w_send, w_recv, load_sem):
+def product_kernel(mid, tile, jobs, have, a_ref, cos_ref, sin_ref, down_ref, across_ref, wq_ref,
+                   wkv_ref, gq_ref, gkv_ref, y_ref, o_ref, keys, values, w, acc, out, held, send,
+                   recv, w_send, w_recv, load_sem):
     _, seq_len, _ = a_ref.shape
     depth = wq_ref.shape[0]
     far_count = gq_ref.shape[0]
@@ -789,6 +790,45 @@
             one.receive(stage)
         done[stage] = max(done[stage], upto)
 
+    group = QUERY_HEADS // KEY_VALUE_HEADS
+    kv_width = keys.shape[1]
+    kv_chunks = -(-2 * kv_width // tile)
+    chunk_heads = tile // HEAD_WIDTH
+    head_count = y_ref.shape[1] // HEAD_WIDTH
+
+    def turn(value):
+        rolled = pltpu.roll(value, HEAD_WIDTH // 2, 1)
+        return (value * cos_ref[...] + rolled * sin_ref[...]).astype(jnp.bfloat16)
+
+    def attend(low, high):
+        def one_head(head, carry):
+            source = pl.multiple_of(2 * kv_width + head * HEAD_WIDTH, HEAD_WIDTH)
+            goal = pl.ds(pl.multiple_of(head * HEAD_WIDTH, HEAD_WIDTH), HEAD_WIDTH)
+            lanes = pl.ds(pl.multiple_of(head // group * HEAD_WIDTH, HEAD_WIDTH), HEAD_WIDTH)
+            scores = lax.dot_general(
+                turn(o_ref[:, pl.ds(source, HEAD_WIDTH)]), keys[:, lanes],
+                (((1,), (1,)), ((), ())), preferred_element_type=jnp.float32,
+            ) * HEAD_WIDTH ** (-0.5)
+            scores = jnp.where(down_ref[...] >= across_ref[...], scores, -1e30)
+            exponentials = jnp.exp(scores - jnp.max(scores, axis=-1, keepdims=True))
+            weights = exponentials / jnp.sum(exponentials, axis=-1, keepdims=True)
+            context = jnp.dot(
+                weights.astype(jnp.bfloat16), values[:, lanes], preferred_element_type=jnp.float32
+            )
+            row_at = lax.broadcasted_iota(jnp.int32, (seq_len, seq_len), 0)
+            home = jnp.where(row_at == across_ref[...], 1.0, 0.0).astype(jnp.bfloat16)
+            ordered = jnp.dot(
+                home, context.astype(jnp.bfloat16), preferred_element_type=jnp.float32
+            )
+            y_ref[:, goal] = ordered.astype(y_ref.dtype)
+            return carry
+
+        if low < high:
+            lax.fori_loop(low, high, one_head, 0)
+
+    def heads_in(upto):
+        return min(head_count, max(0, upto - kv_chunks) * chunk_heads)
+
     for chunk in range(2 * third):
         compute(chunk)
     reduce(0, third)
@@ -798,15 +838,28 @@
         if chunk > 2 * third:
             reduce(1, 2 * third)
         compute(chunk)
+    reduce(1, 2 * third)
+    for lanes in range(0, kv_width, HEAD_WIDTH):
+        part = pl.ds(lanes, HEAD_WIDTH)
+        keys[:, part] = turn(o_ref[:, part])
+    values[...] = o_ref[:, pl.ds(kv_width, kv_width)].astype(values.dtype)
+    ready = heads_in(2 * third)
+    reduce(0, chunks - 2)
+    attend(0, ready // 2)
+    reduce(0, chunks - 1)
+    attend(ready // 2, ready)
     reduce(0, chunks)
+    reduce(1, chunks - 2)
+    attend(ready, heads_in(chunks - 2))
     reduce(1, chunks)
+    attend(max(ready, heads_in(chunks - 2)), head_count)
     for one in sums:
         one.finish()
     for copy in arriving.values():
         copy.wait_send()
 
 
-def product_blocks(a, weights, gathered, tile, jobs, have, mid):
+def product_blocks(a, positions, weights, gathered, tile, jobs, have, mid):
     _, seq_len, depth = a.shape
     columns = sum(one.shape[1] for one in weights)
     chunks = columns // tile
@@ -814,12 +867,23 @@
     anywhere = pl.BlockSpec(memory_space=pltpu.HBM)
     far_count = gathered[0].shape[0]
     dma = pltpu.SemaphoreType.DMA
+    kv_width = weights[0].shape[1] // 2
+    half_width = HEAD_WIDTH // 2
+    exponents = jnp.arange(half_width, dtype=jnp.float32) * (2.0 / HEAD_WIDTH)
+    frequency = rope_base ** (-exponents)
+    angles = positions.astype(jnp.float32)[:, None] * frequency[None, :]
+    cosine, sine = jnp.cos(angles), jnp.sin(angles)
+    cosine = jnp.concatenate([cosine, cosine], axis=1)
+    sine = jnp.concatenate([-sine, sine], axis=1)
     return pl.pallas_call(
         functools.partial(product_kernel, mid, tile, jobs, have),
-        out_shape=jax.ShapeDtypeStruct((seq_len, columns), jnp.float32),
-        in_specs=[vmem] + [anywhere] * 4,
+        out_shape=jax.ShapeDtypeStruct((seq_len, weights[1].shape[1]), jnp.bfloat16),
+        in_specs=[vmem] * 5 + [anywhere] * 4,
         out_specs=vmem,
         scratch_shapes=[
+            pltpu.VMEM((seq_len, columns), jnp.float32),
+            pltpu.VMEM((seq_len, kv_width), jnp.bfloat16),
+            pltpu.VMEM((seq_len, kv_width), jnp.bfloat16),
             pltpu.VMEM((depth, columns), jnp.bfloat16),
             pltpu.VMEM((chunks, NEAR // 2 - 1, seq_len, tile), jnp.float32),
             pltpu.VMEM((chunks, NEAR - 1, seq_len, tile), jnp.bfloat16),
@@ -838,70 +902,7 @@
             bytes_accessed=200 << 20,
             transcendentals=0,
         ),
-    )(a, *weights, *gathered)
-
-
-def attend_kernel(group, q_ref, k_ref, v_ref, cos_ref, sin_ref, down_ref, across_ref, o_ref):
-    cosine, sine = cos_ref[...], sin_ref[...]
-
-    def turn(rows):
-        return (rows * cosine + pltpu.roll(rows, HEAD_WIDTH // 2, 1) * sine).astype(jnp.bfloat16)
-
-    key_rows = turn(k_ref[...])
-    value_rows = v_ref[...].astype(jnp.bfloat16)
-    seq_len = key_rows.shape[0]
-    allowed = down_ref[...] >= across_ref[...]
-    row_at = lax.broadcasted_iota(jnp.int32, (seq_len, seq_len), 0)
-    home = jnp.where(row_at == across_ref[...], 1.0, 0.0).astype(jnp.bfloat16)
-    contexts = []
-    for head in range(group):
-        part = pl.ds(head * HEAD_WIDTH, HEAD_WIDTH)
-        query_rows = turn(q_ref[:, part])
-        scores = lax.dot_general(
-            query_rows, key_rows, (((1,), (1,)), ((), ())), preferred_element_type=jnp.float32
-        ) * HEAD_WIDTH ** (-0.5)
-        scores = jnp.where(allowed, scores, -1e30)
-        exponentials = jnp.exp(scores - jnp.max(scores, axis=-1, keepdims=True))
-        weights = exponentials / jnp.sum(exponentials, axis=-1, keepdims=True)
-        context = jnp.dot(
-            weights.astype(jnp.bfloat16), value_rows, preferred_element_type=jnp.float32
-        )
-        contexts.append(context.astype(jnp.bfloat16))
-    ordered = jnp.dot(
-        home, jnp.concatenate(contexts, axis=1), preferred_element_type=jnp.float32
-    )
-    o_ref[...] = ordered.astype(o_ref.dtype)
-
-
-def attend(product, positions, part_query):
-    seq_len, columns = product.shape
-    group = QUERY_HEADS // KEY_VALUE_HEADS
-    local_kv = part_query // HEAD_WIDTH // group
-    key_at = part_query // HEAD_WIDTH
-    half_width = HEAD_WIDTH // 2
-    exponents = jnp.arange(half_width, dtype=jnp.float32) * (2.0 / HEAD_WIDTH)
-    frequency = rope_base ** (-exponents)
-    angles = positions.astype(jnp.float32)[:, None] * frequency[None, :]
-    cosine, sine = jnp.cos(angles), jnp.sin(angles)
-    cosine = jnp.concatenate([cosine, cosine], axis=1)
-    sine = jnp.concatenate([-sine, sine], axis=1)
-    table = pl.BlockSpec((seq_len, HEAD_WIDTH), lambda g: (0, 0))
-    return pl.pallas_call(
-        functools.partial(attend_kernel, group),
-        grid=(local_kv,),
-        out_shape=jax.ShapeDtypeStruct((seq_len, part_query), jnp.bfloat16),
-        in_specs=[
-            pl.BlockSpec((seq_len, group * HEAD_WIDTH), lambda g: (0, g)),
-            pl.BlockSpec((seq_len, HEAD_WIDTH), lambda g: (0, key_at + g)),
-            pl.BlockSpec((seq_len, HEAD_WIDTH), lambda g: (0, key_at + local_kv + g)),
-            table,
-            table,
-            pl.BlockSpec((seq_len, 1), lambda g: (0, 0)),
-            pl.BlockSpec((1, seq_len), lambda g: (0, 0)),
-        ],
-        out_specs=pl.BlockSpec((seq_len, group * HEAD_WIDTH), lambda g: (0, g)),
-        compiler_params=pltpu.CompilerParams(vmem_limit_bytes=24 << 20),
-    )(product, product, product, cosine, sine, positions[:, None], positions[None, :])
+    )(a, cosine, sine, positions[:, None], positions[None, :], *weights, *gathered)
 
 
 def per_device(
@@ -928,7 +929,7 @@
     t_mid = 1
     far_count = data_count // NEAR
     depth = w_query.shape[0]
-    weights = (w_query, key_value_weight.reshape(depth, -1))
+    weights = (key_value_weight.reshape(depth, -1), w_query)
     tile = math.gcd(256, *(one.shape[1] for one in weights))
     chunks = sum(one.shape[1] for one in weights) // tile
     plan, have = gather_plan(far_count, chunks)
@@ -975,8 +976,9 @@
         text_rows[0], gain[None, :], weights, gathered, tile, plan["sequence"], mid,
         t_mid,
     )
-    product = product_blocks(sequence, weights, gathered, tile, plan["product"], have, mid)
-    context = attend(product, positions, w_query.shape[1])
+    context = product_blocks(
+        sequence, positions, weights, gathered, tile, plan["product"], have, mid
+    )
     return context[None]
 
 

time: 348 us -> 342 us (0.983)
  Pallas kernels: 329 us -> 320 us
    pallas_call x1 -> x0, Pallas kernels: 11.7 us -> none  [attend(): pl.pallas_call(functools.partial(attend_kernel, group), grid=(local_kv,),...]
    unnamed x16 -> x17, local copies, waits for them, and re-layouts: 7.28 us -> 7.79 us
where the time goes in v5:
time: 342 us; the launch traced here: 341 us
  Pallas kernels  320 us (94%)
  local copies, waits for them, and re-layouts  15.2 us (4%)
  other arithmetic  4.73 us (1%)
    pallas_call x1, Pallas kernels, middle_part(): pl.pallas_call(functools.partial(middle_kernel, mid, t_mid, tile, span, w...  125 us
    pallas_call x1, Pallas kernels, product_blocks(): pl.pallas_call(functools.partial(product_kernel, mid, tile, jobs, have),...  123 us
    pallas_call x1, Pallas kernels, front(): pl.pallas_call(functools.partial(front_kernel, mid, w_mid, tile, jobs), o...  72.5 us
    unnamed x17, local copies, waits for them, and re-layouts  7.79 us

profile of v5, /device:TPU:10, one launch (start us, length us, event | category | flops | bytes accessed | tf_op | source)
XLA Modules:
  0.0 341.3 jit_solution(6714429667773904577)
XLA Ops:
  0.0 0.1 sub.63
  0.1 0.7 copy.18
  0.9 0.1 reduce
  1.0 1.3 fusion.2
  2.3 0.1 add.238
  2.4 0.1 add.239
  2.5 0.1 add.247
  2.6 0.1 iota_add_fusion
  2.7 0.1 add.267.pick_ref
  2.8 0.7 add_subtract_fusion
  3.6 0.1 sub.68
  3.6 0.6 broadcast_compare_fusion
  4.3 0.1 add_select_fusion
  4.4 0.1 select_n.148.spot_ref
  4.5 0.8 constant_dynamic-slice_fusion
  5.3 1.5 copy.22
  6.8 0.0 copy-start
  6.8 0.0 copy-start.5
  6.8 0.0 copy-start.1
  6.8 4.6 %copy.17 = bf16[2,200,4096]{2,1,0:T(8,128)(2,1)S(1)} copy(bf16[2,200,4096]{2,0,1:T(2,128)(2,1)} %bitcast.24) | data formatting | bytes 6553600 | tf_op jit(solution)/shard_map/transpose | solution.py:941
  11.4 0.0 copy-start.6
  11.4 72.5 %shard_map.100 = (bf16[4,400,1024]{2,1,0:T(8,128)(2,1)S(1)}, bf16[4,4,64,1600]{3,2,1,0:T(8,128)(2,1)S(1)}, bf16[4,512,1024]{2,1,0:T(8,128)(2,1)}, bf16[4,512,2048]{2,1,0:T(8,128)(2,1)}) custom-call(bf16[2,64,1600]{2,1,0:T(8,128)(2,1)S(1)} %bitcast.22, f32[2,1600]{1,0:T(2,128)S(1)} %get-tuple-element.32.gain_ref, f32[2,1600]{1,0:T(2,128)S(1)} %get-tuple-element.31.bias_ref, ...), custom_call_target="tpu_custom_call" | custom-call | bytes 83886080 | tf_op jit(solution)/shard_map/pallas_call | solution.py:388
  83.9 0.0 copy-start.2
  83.9 1.8 copy-done.2
  85.7 1.8 copy-done.3
  88.1 0.1 broadcast_in_dim.49.rows_ref.down_ref
  88.3 125.2 %shard_map.101 = (bf16[4,384,2048]{2,1,0:T(8,128)(2,1)}, bf16[4,512,1024]{2,1,0:T(8,128)(2,1)}, bf16[4,512,2048]{2,1,0:T(8,128)(2,1)}) custom-call(bf16[4,4,64,1600]{3,2,1,0:T(8,128)(2,1)} %copy-done.2, bf16[1600,1024]{1,0:T(8,128)(2,1)} %bitcast.21, s32[512,1]{1,0:T(8,128)S(1)} %add.267.pick_ref, ...), custom_call_target="tpu_custom_call", output_to_operand_aliasing={{1}: (9, {}), {2}: (10, {})} | custom-call | flops 3355443200 | bytes 104857600 | tf_op jit(solution)/shard_map/pallas_call | solution.py:657
  213.5 0.8 fusion
  214.3 0.9 pad_maximum_fusion
  215.2 0.6 broadcast_in_dim.47.across_ref
  215.8 122.7 %shard_map.102 = bf16[384,2048]{1,0:T(8,128)(2,1)} custom-call(bf16[4,384,2048]{2,1,0:T(8,128)(2,1)} %get-tuple-element.16.a_ref, f32[384,128]{1,0:T(8,128)} %get-tuple-element.33.cos_ref, f32[384,128]{1,0:T(8,128)} %get-tuple-element.34.sin_ref, s32[384,1]{1,0:T(8,128)} %copy-done.4, s32[1,384]{1,0:T(1,128)} %broadcast_in_dim.47.across_ref, ...), custom_call_target="tpu_custom_call" | custom-call | flops 19327352832 | bytes 209715200 | tf_op jit(solution)/shard_map/pallas_call | solution.py:878
  338.6 2.7 copy.29
  (22 shorter events, 0.2 us)
Async XLA Ops:
  6.8 81.5 %copy-start = (bf16[64,8,2,512]{3,1,2,0:T(8,128)(2,1)}, bf16[64,8,2,512]{3,1,2,0:T(8,128)(2,1)S(1)}, u32[]{:S(2)}) copy-start(bf16[64,8,2,512]{3,1,2,0:T(8,128)(2,1)S(1)} %copy.22) | copy-start | bytes 3145732
  6.8 4.6 %copy-start.5 = (bf16[8,8,2,1600]{3,2,1,0:T(2,128)(2,1)S(1)}, bf16[8,8,2,1600]{3,2,1,0:T(2,128)(2,1)}, u32[]{:S(2)}) copy-start(bf16[8,8,2,1600]{3,2,1,0:T(2,128)(2,1)} %param.10) | copy-start | bytes 1228804
  6.8 4.6 %copy-start.1 = (bf16[512,2048]{1,0:T(8,128)(2,1)S(1)}, bf16[512,2048]{1,0:T(8,128)(2,1)}, u32[]{:S(2)}) copy-start(bf16[512,2048]{1,0:T(8,128)(2,1)} %wkv_ref.5) | copy-start | bytes 6291460
  11.4 76.0 %copy-start.6 = (f32[8192]{0:T(1024)S(1)}, f32[8192]{0:T(1024)}, u32[]{:S(2)}) copy-start(f32[8192]{0:T(1024)} %param.15) | copy-start | bytes 98308
  83.9 1.8 copy-start.2
  85.7 1.8 copy-start.3
  88.2 125.3 %copy-start.4 = (s32[384,1]{1,0:T(8,128)}, s32[384,1]{1,0:T(8,128)S(1)}, u32[]{:S(2)}) copy-start(s32[384,1]{1,0:T(8,128)S(1)} %broadcast_in_dim.49.rows_ref.down_ref) | copy-start | bytes 4612
